TPU v7x, 32 devices: a whole 2x2x4 slice. The times are simulated.
32 devices in a mesh: grp: 4 (over x, core), tile: 8 (over z, y).
Axes of the slice: x: 2, y: 2, z: 4, core: 2. Of those that a mesh axis runs over, the one named last changes fastest.
Arguments:
- start_block: float32 [65536, 256], P(('grp', 'tile')), may hold values from -8 to 8
- dense_tiles: float32 [32, 2048, 2048], P(('grp', 'tile')), as said below
- basis: float32 [32, 48, 2048], P(('grp', 'tile')), may hold values from -0.125 to 0.125
- coupling: float32 [4, 8, 48, 1536], P(None, 'tile', None, 'grp'), as said below
- admissible: int32 [4, 8, 32], P(None, 'tile', 'grp'), may hold values from 0 to 1, as said below
Outputs:
- modes: float32 [65536, 256], P(('grp', 'tile'))
Inputs may be any that keep to these rules, and one draw needn't show every extreme that they name: admissible is symmetric over tile pairs (the entry for row tile i and column tile j equals that for row tile j and column tile i) and 0 where the row tile equals the column tile. `dense_tiles`: each dense tile is symmetric: a positive scale times a diagonal plus an unstructured symmetric off-diagonal part. The coupling, read as a matrix of order 32 * 48, is symmetric: block S_ji is the transpose of S_ij.
All inputs are finite; a program needn't handle non-finite values.
Results may differ from a plain program's by a relative error of at most 0.0003.
Values sent between devices are 32-bit elements; how exact they have to be, the bound alone decides.
No kernel may reach another device: no remote copies, remote signals or barrier semaphores. Data moves between devices by JAX's collectives and lax.ppermute only.
A program may use at most 128 MiB of HBM per device.

v0:
```python
import functools

import jax
import jax.numpy as jnp
from jax import lax
from jax.experimental import pallas as pl
from jax.experimental.pallas import tpu as pltpu
from jax.sharding import PartitionSpec as P


HP = lax.Precision.HIGHEST
SMEM = pl.BlockSpec(memory_space=pltpu.SMEM)
VMEM = pl.BlockSpec(memory_space=pltpu.VMEM)
VREG = (8, 128)


def down(x, row):
    return jnp.broadcast_to(x[row : row + 1, :], VREG)


def factor_inverse(t_ref, out_ref):
    n = t_ref.shape[0]
    halves = range(n // 128)
    lane = lax.broadcasted_iota(jnp.int32, VREG, 1)
    sub = lax.broadcasted_iota(jnp.int32, VREG, 0)
    every = sub < 8
    rows = [t_ref[:8, 128 * g : 128 * g + 128] for g in halves]
    for k in range(0, n, 8):
        h, at = k // 128, k % 128
        cols = [jnp.where(every, jnp.broadcast_to(rows[h][:, at + c : at + c + 1], VREG), 0.0) for c in range(8)]
        inside = (lane >= at) & (lane < at + 8)
        rows[h] = jnp.where(inside, jnp.where(lane - at == sub, 1.0, 0.0), rows[h])
        pivots = jnp.ones(VREG, jnp.float32)
        done = list(rows)
        for j in range(8):
            pivot = down(cols[j], j)
            pivots = jnp.where(sub == j, pivot, pivots)
            f = jnp.where(sub == j, 0.0, cols[j])
            for c in range(j + 1, 8):
                cols[c] = cols[c] - (f * down(cols[c], j)) / pivot
            for g in halves:
                done[g] = jnp.where(sub == j, rows[g], done[g])
                rows[g] = rows[g] - (f * down(rows[g], j)) / pivot
        roots = lax.rsqrt(pivots)
        for g in halves:
            if g > h:
                out = jnp.zeros(VREG, jnp.float32)
            else:
                out = done[g] * roots
                if g == h:
                    out = jnp.where(lane < at + 8, out, 0.0)
            out_ref[k : k + 8, 128 * g : 128 * g + 128] = out
        if k + 8 == n:
            break
        rows = [x / pivots for x in rows]
        wide = [[down(rows[g], i) for i in range(8)] for g in halves]
        for r in range(k + 8, n, 8):
            now = [t_ref[r : r + 8, 128 * g : 128 * g + 128] for g in halves]
            f = [jnp.broadcast_to(now[h][:, at + i : at + i + 1], VREG) for i in range(8)]
            now[h] = jnp.where(inside, 0.0, now[h])
            for g in halves:
                w = wide[g]
                low = (f[0] * w[0] + f[1] * w[1]) + (f[2] * w[2] + f[3] * w[3])
                high = (f[4] * w[4] + f[5] * w[5]) + (f[6] * w[6] + f[7] * w[7])
                now[g] = now[g] - (low + high)
            if r == k + 8:
                rows = now
            else:
                for g in halves:
                    t_ref[r : r + 8, 128 * g : 128 * g + 128] = now[g]


def split(x, parts):
    terms = []
    for at in range(parts):
        terms.append(x.astype(jnp.bfloat16))
        if at + 1 < parts:
            x = x - terms[-1].astype(jnp.float32)
    return terms


def mul(a, b, contract=(1, 0)):
    return lax.dot_general(a, b, (((contract[0],), (contract[1],)), ((), ())), preferred_element_type=jnp.float32)


def triangle_masks(m):
    row = lax.broadcasted_iota(jnp.int32, (m, m), 0)
    col = lax.broadcasted_iota(jnp.int32, (m, m), 1)
    return row, col


def pack_into(side_ref, gram, mine_ref, theirs_ref):
    m = gram.shape[0] // 2
    row, col = triangle_masks(m)
    second = gram[m:, m:]
    cross = gram[m:, :m]
    both = jnp.where(row >= col, gram[:m, :m], second)
    diag = jnp.sum(jnp.where(row == col, second, 0.0), axis=0, keepdims=True)
    south = side_ref[0] == 0
    mine_ref[:m] = jnp.where(south, cross, both)
    theirs_ref[:m] = jnp.where(south, both, cross)
    mine_ref[m:] = jnp.broadcast_to(diag, (8, m))
    theirs_ref[m:] = jnp.broadcast_to(diag, (8, m))


def unpack_into(scale, side_ref, mine_ref, theirs_ref, t_ref):
    m = mine_ref.shape[1]
    row, col = triangle_masks(m)
    south = side_ref[0] == 0
    cross = jnp.where(south, mine_ref[:m], theirs_ref[:m]) * scale
    both = jnp.where(south, theirs_ref[:m], mine_ref[:m]) * scale
    diag = jnp.where(south, theirs_ref[m : m + 1], mine_ref[m : m + 1]) * scale
    flip = both.T
    t_ref[:m, :m] = jnp.where(row >= col, both, flip)
    t_ref[m:, m:] = jnp.where(row == col, jnp.broadcast_to(diag, (m, m)), jnp.where(row < col, both, flip))
    t_ref[m:, :m] = cross
    t_ref[:m, m:] = cross.T


def stack_basis(basis_ref, stacked):
    width = basis_ref.shape[0]
    high, low = split(basis_ref[...], 2)
    for at, part in enumerate((high, low, high, high, low)):
        stacked[at * width : (at + 1) * width] = part


def stack_sums(summed_ref):
    high, mid, low = split(summed_ref[...], 3)
    return jnp.concatenate([high, high, mid, low, mid], axis=0)


def gram_terms(field, total, cross):
    high, mid = split(field, 2)
    total[...] += mul(high, high, (0, 0)) + mul(mid, mid, (0, 0))
    cross[...] += mul(high, mid, (0, 0))


CHUNK = 512


def chunks(rows, step):
    def run(at, carry):
        step(pl.ds(pl.multiple_of(at * CHUNK, CHUNK), CHUNK))
        return carry

    lax.fori_loop(0, rows // CHUNK, run, 0)


def piece_rows(pieces, step):
    start = 0
    for piece in pieces:
        step(pl.ds(start, piece.shape[0]), piece)
        start += piece.shape[0]


def mix_kernel(side_ref, basis_ref, summed_ref, *refs):
    pieces, (image_ref, coeffs_ref, mine_ref, theirs_ref, stacked, total, cross, parts) = refs[:-8], refs[-8:]
    width = basis_ref.shape[0]
    stack_basis(basis_ref, stacked)
    sums = stack_sums(summed_ref)
    total[...] = jnp.zeros_like(total)
    cross[...] = jnp.zeros_like(cross)
    parts[...] = jnp.zeros_like(parts)

    def step(rows, piece):
        image = piece[...] + mul(stacked[:, rows], sums, (0, 0))
        image_ref[rows, :] = image
        high, mid, low = split(image, 3)
        total[...] += mul(high, high, (0, 0)) + mul(mid, mid, (0, 0))
        cross[...] += mul(high, mid, (0, 0))
        two = stacked[: 2 * width, rows]
        both = mul(two, high) + mul(two, mid)
        parts[...] += both[:width] + both[width:] + mul(two[:width], low)

    piece_rows(pieces, step)
    coeffs_ref[...] = parts[...]
    pack_into(side_ref, total[...] + (cross[...] + cross[...].T), mine_ref, theirs_ref)


def mix(side, pieces, basis, summed):
    rows, modes = basis.shape[1], summed.shape[1]
    width = basis.shape[0]
    part = jax.ShapeDtypeStruct((modes // 2 + 8, modes // 2), jnp.float32)
    square = pltpu.VMEM((modes, modes), jnp.float32)
    return pl.pallas_call(
        mix_kernel,
        out_shape=(jax.ShapeDtypeStruct((rows, modes), jnp.float32), jax.ShapeDtypeStruct((width, modes), jnp.float32), part, part),
        in_specs=[SMEM, VMEM, VMEM] + [VMEM] * len(pieces), out_specs=(VMEM,) * 4,
        scratch_shapes=[pltpu.VMEM((5 * width, rows), jnp.bfloat16), square, square, pltpu.VMEM((width, modes), jnp.float32)],
        name="mix", compiler_params=pltpu.CompilerParams(vmem_limit_bytes=24 * 2**20), cost_estimate=pl.CostEstimate(flops=12 * rows * modes * modes, bytes_accessed=8 * rows * modes, transcendentals=0),
    )(side, basis, summed, *pieces)


def factor_kernel(scale, side_ref, mine_ref, theirs_ref, out_ref, t_ref):
    unpack_into(scale, side_ref, mine_ref, theirs_ref, t_ref)
    factor_inverse(t_ref, out_ref)


def factor(side, mine, theirs, scale):
    modes = 2 * mine.shape[1]
    return pl.pallas_call(
        functools.partial(factor_kernel, scale),
        out_shape=jax.ShapeDtypeStruct((modes, modes), jnp.float32),
        in_specs=[SMEM, VMEM, VMEM], out_specs=VMEM, scratch_shapes=[pltpu.VMEM((modes, modes), jnp.float32)],
        name="factor", compiler_params=pltpu.CompilerParams(vmem_limit_bytes=16 * 2**20),
        cost_estimate=pl.CostEstimate(flops=40_000_000, bytes_accessed=8 * modes * modes, transcendentals=0),
    )(side, mine, theirs)


def middle_kernel(side_ref, inverse, basis_ref, summed_ref, *refs):
    pieces, (image_ref, out_mine_ref, out_theirs_ref, stacked, total, cross) = refs[:-6], refs[-6:]
    stack_basis(basis_ref, stacked)
    sums = stack_sums(summed_ref)
    total[...] = jnp.zeros_like(total)
    cross[...] = jnp.zeros_like(cross)
    first, second = split(inverse[...], 2)

    def step(rows, piece):
        further = piece[...] + mul(stacked[:, rows], sums, (0, 0))
        high, mid, low = split(further, 3)
        image = (mul(high, first, (1, 1)) + mul(mid, first, (1, 1))) + (mul(high, second, (1, 1)) + (mul(mid, second, (1, 1)) + mul(low, first, (1, 1))))
        image_ref[rows, :] = image
        gram_terms(image, total, cross)

    piece_rows(pieces, step)
    pack_into(side_ref, total[...] + (cross[...] + cross[...].T), out_mine_ref, out_theirs_ref)


def middle(side, inverse, pieces, basis, summed):
    rows, modes = basis.shape[1], summed.shape[1]
    width = basis.shape[0]
    part = jax.ShapeDtypeStruct((modes // 2 + 8, modes // 2), jnp.float32)
    square = pltpu.VMEM((modes, modes), jnp.float32)
    return pl.pallas_call(
        middle_kernel,
        out_shape=(jax.ShapeDtypeStruct((rows, modes), jnp.float32), part, part),
        in_specs=[SMEM] + [VMEM] * (3 + len(pieces)), out_specs=(VMEM,) * 3,
        scratch_shapes=[pltpu.VMEM((5 * width, rows), jnp.bfloat16), square, square],
        name="middle", compiler_params=pltpu.CompilerParams(vmem_limit_bytes=28 * 2**20), cost_estimate=pl.CostEstimate(flops=20 * rows * modes * modes, bytes_accessed=8 * rows * modes, transcendentals=0),
    )(side, inverse, basis, summed, *pieces)


def last_kernel(inverse, image_ref, out_ref):
    first, second = split(inverse[...], 2)

    def step(rows):
        high, mid = split(image_ref[rows, :], 2)
        out_ref[rows, :] = mul(high, first, (1, 1)) + (mul(mid, first, (1, 1)) + (mul(high, second, (1, 1)) + mul(mid, second, (1, 1))))

    chunks(image_ref.shape[0], step)


def last(inverse, image):
    return pl.pallas_call(
        last_kernel,
        out_shape=jax.ShapeDtypeStruct(image.shape, jnp.float32),
        in_specs=[VMEM] * 2, out_specs=VMEM,
        name="last", compiler_params=pltpu.CompilerParams(vmem_limit_bytes=20 * 2**20), cost_estimate=pl.CostEstimate(flops=8 * image.size * image.shape[1], bytes_accessed=8 * image.size, transcendentals=0),
    )(inverse, image)


BLOCK = 256
ONE = (2, 2, 2, 2)
TWO = (2, 3, 3)


def near_rows(start, dense_ref, high, mid, low, out_ref, held, sems):
    count = out_ref.shape[0] // BLOCK

    def copy(at):
        return pltpu.make_async_copy(dense_ref.at[pl.ds(start + at * BLOCK, BLOCK)], held.at[at], sems.at[at])

    for at in range(count):
        copy(at).start()

    def run(at, carry):
        copy(at).wait()
        top, rest = split(held[at], 2)
        out_ref[pl.ds(pl.multiple_of(at * BLOCK, BLOCK), BLOCK)] = mul(top, high[...]) + (
            mul(top, mid[...]) + (mul(rest, high[...]) + (mul(rest, mid[...]) + mul(top, low[...])))
        )
        return carry

    lax.fori_loop(0, count, run, 0)


def near_first_kernel(dense_ref, field_ref, out_ref, high, mid, low, held, sems):
    def run(at, carry):
        rows = pl.ds(pl.multiple_of(at * BLOCK, BLOCK), BLOCK)
        high[rows, :], mid[rows, :], low[rows, :] = split(field_ref[rows, :], 3)
        return carry

    lax.fori_loop(0, field_ref.shape[0] // BLOCK, run, 0)
    near_rows(0, dense_ref, high, mid, low, out_ref, held, sems)


def near_next_kernel(start, dense_ref, high, mid, low, out_ref, held, sems):
    near_rows(start, dense_ref, high, mid, low, out_ref, held, sems)


def near_of(dense, field, shares):
    rows, depth = dense.shape
    modes = field.shape[1]
    sizes = [rows * share // sum(shares) for share in shares]
    term = jax.ShapeDtypeStruct(field.shape, jnp.bfloat16)
    anywhere = pl.BlockSpec(memory_space=pltpu.HBM)
    pieces, terms, start = [], (), 0
    for at, size in enumerate(sizes):
        out = jax.ShapeDtypeStruct((size, modes), jnp.float32)
        count = size // BLOCK
        settings = dict(
            scratch_shapes=[pltpu.VMEM((count, BLOCK, depth), jnp.float32), pltpu.SemaphoreType.DMA((count,))],
            compiler_params=pltpu.CompilerParams(vmem_limit_bytes=50 * 2**20),
            cost_estimate=pl.CostEstimate(flops=10 * size * depth * modes, bytes_accessed=4 * size * depth, transcendentals=0),
        )
        if at == 0:
            piece, *terms = pl.pallas_call(
                near_first_kernel, out_shape=(out, term, term, term), in_specs=[anywhere, VMEM], out_specs=(VMEM,) * 4,
                name="near_first", **settings,
            )(dense, field)
        else:
            piece = pl.pallas_call(
                functools.partial(near_next_kernel, start), out_shape=out, in_specs=[anywhere, VMEM, VMEM, VMEM],
                out_specs=VMEM, name="near_next", **settings,
            )(dense, *terms)
        pieces.append(piece)
        start += size
    return pieces


def couple_kernel(order, place_ref, masked_ref, *refs):
    blocks, far_ref, near_ref, held = refs[: len(order)], refs[-3], refs[-2], refs[-1]
    tile, group = place_ref[0], place_ref[1]
    width = blocks[0].shape[0] // len(order[0])
    for names, block in zip(order, blocks):
        for at, name in enumerate(names):
            start = pl.multiple_of((tile ^ name) * width, 8)
            held[pl.ds(start, width), :] = block[at * width : (at + 1) * width, :]
    total = jnp.dot(masked_ref[...], held[...], precision=HP, preferred_element_type=jnp.float32)
    held[: total.shape[0], :] = total
    groups = total.shape[0] // width
    count = groups // 2
    for at in range(count):
        near_ref[at * width : (at + 1) * width] = held[pl.ds(pl.multiple_of((group ^ at) * width, 8), width), :]
        far_ref[at * width : (at + 1) * width] = held[pl.ds(pl.multiple_of((group ^ (at + count)) * width, 8), width), :]


def couple(place, masked, blocks, order):
    rows, depth = masked.shape
    modes = blocks[0].shape[1]
    half = jax.ShapeDtypeStruct((rows // 2, modes), jnp.float32)
    return pl.pallas_call(
        functools.partial(couple_kernel, order),
        out_shape=(half, half), in_specs=[SMEM, VMEM] + [VMEM] * len(blocks), out_specs=(VMEM, VMEM),
        scratch_shapes=[pltpu.VMEM((max(rows, depth), modes), jnp.float32)], name="couple", compiler_params=pltpu.CompilerParams(vmem_limit_bytes=8 * 2**20),
        cost_estimate=pl.CostEstimate(flops=12 * rows * depth * modes, bytes_accessed=4 * rows * depth, transcendentals=0),
    )(place, masked, *blocks)


def swap(x, axis, bit):
    return lax.ppermute(x, axis, [(i, i ^ bit) for i in range(lax.axis_size(axis))])


def body(start_block, dense_tiles, basis, coupling, admissible):
    groups = coupling.shape[0]
    width = basis.shape[1]
    span = coupling.shape[3] // width
    tiles = lax.axis_size("tile")
    total_rows = lax.axis_size("grp") * tiles * start_block.shape[0]
    flags = admissible.astype(jnp.float32).reshape(groups, 1, span, 1)
    masked = (coupling.reshape(groups, width, span, width) * flags).reshape(groups * width, span * width)
    dense = dense_tiles[0]
    rows_basis = basis[0]
    group, tile = lax.axis_index("grp"), lax.axis_index("tile")
    place = jnp.stack([tile, group]).astype(jnp.int32)
    side = jnp.stack([group % 2]).astype(jnp.int32)

    def couple_all(coeffs):
        blocks, order, held, names = [coeffs], [(0,)], coeffs, (0,)
        bit = tiles // 2
        while bit:
            got = swap(held, "tile", bit)
            blocks.append(got)
            order.append(tuple(name ^ bit for name in names))
            names = names + order[-1]
            bit //= 2
            if bit:
                held = jnp.concatenate([held, got])
        far, near = couple(place, masked, blocks, tuple(order))
        bit = groups // 2
        while True:
            got = swap(far, "grp", bit)
            near = near + got
            bit //= 2
            if not bit:
                return near
            far, near = near[near.shape[0] // 2 :], near[: near.shape[0] // 2]

    scale = 1.0 / total_rows

    def add_devices(mine, theirs):
        mine = mine + swap(theirs, "grp", 1)
        for axis, bit in sum_rounds(groups, tiles):
            got = swap(mine, axis, bit)
            mine = mine + got
        return mine, swap(mine, "grp", 1)

    summed = couple_all(jnp.dot(rows_basis, start_block, precision=HP))
    image, coeffs, mine, theirs = mix(side, near_of(dense, start_block, ONE), rows_basis, summed)
    mine, theirs = add_devices(mine, theirs)
    summed = couple_all(coeffs)
    image, mine, theirs = middle(side, factor(side, mine, theirs, scale), near_of(dense, image, TWO), rows_basis, summed)
    mine, theirs = add_devices(mine, theirs)
    return last(factor(side, mine, theirs, scale), image)


def sum_rounds(groups, tiles):
    rounds = []
    bit = groups // 2
    while bit > 1:
        rounds.append(("grp", bit))
        bit //= 2
    bit = 1
    while bit < tiles:
        rounds.append(("tile", bit))
        bit *= 2
    return rounds


def solution(mesh):
    placed = (
        P(("grp", "tile"), None),
        P(("grp", "tile"), None, None),
        P(("grp", "tile"), None, None),
        P(None, "tile", None, "grp"),
        P(None, "tile", "grp"),
    )
    return jax.shard_map(body, mesh=mesh, in_specs=placed, out_specs=P(("grp", "tile"), None), check_vma=False)
```

profile of v0, /device:TPU:0, one launch (start us, length us, event | category | flops | bytes accessed | tf_op | source)
XLA Modules:
  0.0 143.6 jit_solution(10497241841076518613)
XLA Ops:
  0.0 2.8 %fusion.refs_0_ = f32[48,256]{1,0:T(8,128)S(1)} fusion(f32[2048,256]{1,0:T(8,128)} %field_ref.1, f32[1,48,2048]{2,1,0:T(8,128)} %param.7), kind=kOutput, calls=%fused_computation.8 | convolution fusion | flops 301989888 | bytes 2539520 | tf_op jit(solution)/shard_map/dot_general | solution.py:408
  2.8 4.1 %collective-permute-start = (f32[48,256]{1,0:T(8,128)S(1)}, f32[48,256]{1,0:T(8,128)S(1)}, u32[]{:S(2)}, u32[]{:S(2)}) collective-permute-start(f32[48,256]{1,0:T(8,128)S(1)} %fusion.refs_0_), channel_id=1, source_target_pairs={{0,4},{1,5},{2,6},{3,7},{4,0},{5,1},{6,2},{7,3},{8,12},{9,13},{10,... | collective-permute-start | bytes 147464 | tf_op jit(solution)/shard_map/ppermute | solution.py:361
  7.0 6.9 %near_first.2 = (f32[512,256]{1,0:T(8,128)S(1)}, bf16[2048,256]{1,0:T(8,128)(2,1)S(1)}, bf16[2048,256]{1,0:T(8,128)(2,1)S(1)}, bf16[2048,256]{1,0:T(8,128)(2,1)S(1)}) custom-call(f32[2048,2048]{1,0:T(8,128)} %bitcast.15, f32[2048,256]{1,0:T(8,128)} %field_ref.1), custom_call_target="tpu_custom_call" | custom-call | flops 2684354560 | bytes 4194304 | tf_op jit(solution)/shard_map/near_first/pallas_call | solution.py:317
  13.9 0.8 copy-done.10
  14.7 4.8 %near_next.7.refs_3_ = f32[512,256]{1,0:T(8,128)S(1)} custom-call(f32[2048,2048]{1,0:T(8,128)} %bitcast.16, bf16[2048,256]{1,0:T(8,128)(2,1)S(1)} %get-tuple-element.27.high, bf16[2048,256]{1,0:T(8,128)(2,1)S(1)} %get-tuple-element.28.mid, bf16[2048,256]{1,0:T(8,128)(2,1)S(1)} %get-tuple-element.29.low), custom_call_target="tpu_custom_call" | custom-call | flops 2684354560 | bytes 4194304 | tf_op jit(solution)/shard_map/near_next/pallas_call | solution.py:322
  19.5 0.8 copy-done.1
  20.3 1.0 mul.14
  21.3 2.1 %mul.15 = f32[192,384]{1,0:T(8,128)} reshape(f32[4,48,8,48]{3,2,1,0:T(8,128)} %mul.14) | data formatting | bytes 589824 | tf_op jit(solution)/shard_map/mul | solution.py:371
  23.4 1.6 %collective-permute-start.1 = (f32[96,256]{1,0:T(8,128)S(1)}, f32[96,256]{1,0:T(8,128)S(1)}, u32[]{:S(2)}, u32[]{:S(2)}) collective-permute-start(f32[96,256]{1,0:T(8,128)S(1)} %pad_maximum_fusion.2), channel_id=1, source_target_pairs={{0,2},{1,3},{2,0},{3,1},{4,6},{5,7},{6,4},{7,5},{8,10},{9,11},{10,... | collective-permute-start | bytes 294920 | tf_op jit(solution)/shard_map/ppermute | solution.py:361
  25.0 0.1 pad_add_fusion.place_ref
  25.1 3.0 %collective-permute-done.1.refs_2_ = f32[96,256]{1,0:T(8,128)S(1)} collective-permute-done((f32[96,256]{1,0:T(8,128)S(1)}, f32[96,256]{1,0:T(8,128)S(1)}, u32[]{:S(2)}, u32[]{:S(2)}) %collective-permute-start.1) | collective-permute-done | bytes 98336 | tf_op jit(solution)/shard_map/ppermute | solution.py:361
  28.1 1.6 %collective-permute-start.2 = (f32[192,256]{1,0:T(8,128)S(1)}, f32[192,256]{1,0:T(8,128)S(1)}, u32[]{:S(2)}, u32[]{:S(2)}) collective-permute-start(f32[192,256]{1,0:T(8,128)S(1)} %pad_maximum_fusion), channel_id=1, source_target_pairs={{0,1},{1,0},{2,3},{3,2},{4,5},{5,4},{6,7},{7,6},{8,9},{9,8},{10,11... | collective-permute-start | bytes 589832 | tf_op jit(solution)/shard_map/ppermute | solution.py:361
  29.7 1.1 bitcast_multiply_fusion.masked_ref
  30.8 3.0 %collective-permute-done.2.refs_3_ = f32[192,256]{1,0:T(8,128)S(1)} collective-permute-done((f32[192,256]{1,0:T(8,128)S(1)}, f32[192,256]{1,0:T(8,128)S(1)}, u32[]{:S(2)}, u32[]{:S(2)}) %collective-permute-start.2) | collective-permute-done | bytes 196640 | tf_op jit(solution)/shard_map/ppermute | solution.py:361
  33.8 1.1 couple.2
  34.9 1.6 %collective-permute-start.3 = (f32[96,256]{1,0:T(8,128)S(1)}, f32[96,256]{1,0:T(8,128)S(1)}, u32[]{:S(2)}, u32[]{:S(2)}) collective-permute-start(f32[96,256]{1,0:T(8,128)S(1)} %get-tuple-element.25), channel_id=1, source_target_pairs={{0,16},{8,24},{16,0},{24,8},{1,17},{9,25},{17,1},{25,9},{2,18},{10... | collective-permute-start | bytes 294920 | tf_op jit(solution)/shard_map/ppermute | solution.py:361
  36.5 4.8 %near_next.6.refs_2_ = f32[512,256]{1,0:T(8,128)S(1)} custom-call(f32[2048,2048]{1,0:T(8,128)} %bitcast.17, bf16[2048,256]{1,0:T(8,128)(2,1)S(1)} %get-tuple-element.27.high, bf16[2048,256]{1,0:T(8,128)(2,1)S(1)} %get-tuple-element.28.mid, bf16[2048,256]{1,0:T(8,128)(2,1)S(1)} %get-tuple-element.29.low), custom_call_target="tpu_custom_call" | custom-call | flops 2684354560 | bytes 4194304 | tf_op jit(solution)/shard_map/near_next/pallas_call | solution.py:322
  41.3 0.8 copy-done.3
  42.1 0.6 copy-done.12
  42.7 0.6 slice.17
  43.4 4.8 %near_next.5.refs_1_ = f32[512,256]{1,0:T(8,128)S(1)} custom-call(f32[2048,2048]{1,0:T(8,128)} %bitcast.18, bf16[2048,256]{1,0:T(8,128)(2,1)S(1)} %get-tuple-element.27.high, bf16[2048,256]{1,0:T(8,128)(2,1)S(1)} %get-tuple-element.28.mid, bf16[2048,256]{1,0:T(8,128)(2,1)S(1)} %get-tuple-element.29.low), custom_call_target="tpu_custom_call" | custom-call | flops 2684354560 | bytes 4194304 | tf_op jit(solution)/shard_map/near_next/pallas_call | solution.py:322
  48.2 0.0 copy-start.5
  48.2 0.8 copy-done.5
  49.0 0.8 slice_add_fusion.1.summed_ref
  49.9 1.0 copy-done.2
  50.9 1.0 copy-done.4
  51.9 1.0 copy-done.6
  53.0 1.0 copy-done.11
  54.0 2.3 %mix.1 = (f32[2048,256]{1,0:T(8,128)S(1)}, f32[48,256]{1,0:T(8,128)S(1)}, f32[136,128]{1,0:T(8,128)S(1)}, f32[136,128]{1,0:T(8,128)S(1)}) custom-call(s32[1]{0:T(128)} %bitcast.side_ref, f32[48,2048]{1,0:T(8,128)S(1)} %bitcast.13, f32[48,256]{1,0:T(8,128)S(1)} %slice_add_fusion.1.summed_ref, f32[512,256]{1,0:T(8,128)S(1)} %copy-done.11, ...), custom_call_target="tpu_custom_call" | custom-call | flops 1610612736 | bytes 4194304 | tf_op jit(solution)/shard_map/mix/pallas_call | solution.py:185
  56.3 1.3 copy-done
  57.6 0.3 collective-permute-start.11
  57.9 0.2 collective-permute-start.5
  58.1 4.5 %collective-permute-done.11.refs_1_ = f32[48,256]{1,0:T(8,128)S(1)} collective-permute-done((f32[48,256]{1,0:T(8,128)S(1)}, f32[48,256]{1,0:T(8,128)S(1)}, u32[]{:S(2)}, u32[]{:S(2)}) %collective-permute-start.11) | collective-permute-done | bytes 49184 | tf_op jit(solution)/shard_map/ppermute | solution.py:361
  62.6 1.7 %collective-permute-start.12 = (f32[96,256]{1,0:T(8,128)S(1)}, f32[96,256]{1,0:T(8,128)S(1)}, u32[]{:S(2)}, u32[]{:S(2)}) collective-permute-start(f32[96,256]{1,0:T(8,128)S(1)} %pad_maximum_fusion.3), channel_id=1, source_target_pairs={{0,2},{1,3},{2,0},{3,1},{4,6},{5,7},{6,4},{7,5},{8,10},{9,11},{10,... | collective-permute-start | bytes 294920 | tf_op jit(solution)/shard_map/ppermute | solution.py:361
  64.3 0.6 collective-permute-start.6
  64.9 3.8 %collective-permute-done.6 = f32[136,128]{1,0:T(8,128)S(1)} collective-permute-done((f32[136,128]{1,0:T(8,128)S(1)}, f32[136,128]{1,0:T(8,128)S(1)}, u32[]{:S(2)}, u32[]{:S(2)}) %collective-permute-start.6) | collective-permute-done | bytes 69664 | tf_op jit(solution)/shard_map/ppermute | solution.py:361
  68.7 1.6 %collective-permute-start.7 = (f32[136,128]{1,0:T(8,128)S(1)}, f32[136,128]{1,0:T(8,128)S(1)}, u32[]{:S(2)}, u32[]{:S(2)}) collective-permute-start(f32[136,128]{1,0:T(8,128)S(1)} %add.50), channel_id=1, source_target_pairs={{0,1},{1,0},{2,3},{3,2},{4,5},{5,4},{6,7},{7,6},{8,9},{9,8},{10,11... | collective-permute-start | bytes 208904 | tf_op jit(solution)/shard_map/ppermute | solution.py:361
  70.3 0.6 collective-permute-start.13
  70.9 2.9 %collective-permute-done.7 = f32[136,128]{1,0:T(8,128)S(1)} collective-permute-done((f32[136,128]{1,0:T(8,128)S(1)}, f32[136,128]{1,0:T(8,128)S(1)}, u32[]{:S(2)}, u32[]{:S(2)}) %collective-permute-start.7) | collective-permute-done | bytes 69664 | tf_op jit(solution)/shard_map/ppermute | solution.py:361
  73.8 0.4 collective-permute-start.8
  74.2 6.8 %near_first.3 = (f32[512,256]{1,0:T(8,128)S(1)}, bf16[2048,256]{1,0:T(8,128)(2,1)S(1)}, bf16[2048,256]{1,0:T(8,128)(2,1)S(1)}, bf16[2048,256]{1,0:T(8,128)(2,1)S(1)}) custom-call(f32[2048,2048]{1,0:T(8,128)} %bitcast.19, f32[2048,256]{1,0:T(8,128)} %copy-done), custom_call_target="tpu_custom_call" | custom-call | flops 2684354560 | bytes 4194304 | tf_op jit(solution)/shard_map/near_first/pallas_call | solution.py:317
  81.0 1.0 collective-permute-start.9
  82.1 1.1 couple.3
  83.1 0.5 collective-permute-start.14
  83.7 6.2 %near_next.9.refs_2_ = f32[768,256]{1,0:T(8,128)S(1)} custom-call(f32[2048,2048]{1,0:T(8,128)} %bitcast.20, bf16[2048,256]{1,0:T(8,128)(2,1)S(1)} %get-tuple-element.37.high, bf16[2048,256]{1,0:T(8,128)(2,1)S(1)} %get-tuple-element.38.mid, bf16[2048,256]{1,0:T(8,128)(2,1)S(1)} %get-tuple-element.39.low), custom_call_target="tpu_custom_call" | custom-call | flops 4026531840 | bytes 6291456 | tf_op jit(solution)/shard_map/near_next/pallas_call | solution.py:322
  89.9 0.1 collective-permute-start.10
  90.0 0.5 collective-permute-start.15
  90.6 6.2 %near_next.8.refs_1_ = f32[768,256]{1,0:T(8,128)S(1)} custom-call(f32[2048,2048]{1,0:T(8,128)} %bitcast.21, bf16[2048,256]{1,0:T(8,128)(2,1)S(1)} %get-tuple-element.37.high, bf16[2048,256]{1,0:T(8,128)(2,1)S(1)} %get-tuple-element.38.mid, bf16[2048,256]{1,0:T(8,128)(2,1)S(1)} %get-tuple-element.39.low), custom_call_target="tpu_custom_call" | custom-call | flops 4026531840 | bytes 6291456 | tf_op jit(solution)/shard_map/near_next/pallas_call | solution.py:322
  96.8 8.8 %factor.2.inverse = f32[256,256]{1,0:T(8,128)S(1)} custom-call(s32[1]{0:T(128)} %bitcast.side_ref, f32[136,128]{1,0:T(8,128)S(1)} %add.53.mine_ref, f32[136,128]{1,0:T(8,128)S(1)} %collective-permute-done.10.theirs_ref), custom_call_target="tpu_custom_call" | custom-call | flops 40000000 | bytes 524288 | tf_op jit(solution)/shard_map/factor/pallas_call | solution.py:201
  105.6 4.4 %middle.1 = (f32[2048,256]{1,0:T(8,128)S(1)}, f32[136,128]{1,0:T(8,128)S(1)}, f32[136,128]{1,0:T(8,128)S(1)}) custom-call(s32[1]{0:T(128)} %bitcast.side_ref, f32[256,256]{1,0:T(8,128)S(1)} %factor.2.inverse, f32[48,2048]{1,0:T(8,128)S(1)} %bitcast.14, f32[48,256]{1,0:T(8,128)S(1)} %slice_add_fusion.summed_ref, f32[512,256]{1,0:T(8,128)S(1)} %get-tuple-element.36.refs_0_, ...), custom_call_target="tpu_custom_call" | custom-call | flops 2684354560 | bytes 4194304 | tf_op jit(solution)/shard_map/middle/pallas_call | solution.py:234
  110.0 0.1 collective-permute-start.16
  110.1 1.2 collective-permute-done.16
  111.4 1.6 %collective-permute-start.17 = (f32[136,128]{1,0:T(8,128)S(1)}, f32[136,128]{1,0:T(8,128)S(1)}, u32[]{:S(2)}, u32[]{:S(2)}) collective-permute-start(f32[136,128]{1,0:T(8,128)S(1)} %add.56), channel_id=1, source_target_pairs={{0,16},{8,24},{16,0},{24,8},{1,17},{9,25},{17,1},{25,9},{2,18},{10... | collective-permute-start | bytes 208904 | tf_op jit(solution)/shard_map/ppermute | solution.py:361
  113.0 2.8 %collective-permute-done.17 = f32[136,128]{1,0:T(8,128)S(1)} collective-permute-done((f32[136,128]{1,0:T(8,128)S(1)}, f32[136,128]{1,0:T(8,128)S(1)}, u32[]{:S(2)}, u32[]{:S(2)}) %collective-permute-start.17) | collective-permute-done | bytes 69664 | tf_op jit(solution)/shard_map/ppermute | solution.py:361
  115.8 1.6 %collective-permute-start.18 = (f32[136,128]{1,0:T(8,128)S(1)}, f32[136,128]{1,0:T(8,128)S(1)}, u32[]{:S(2)}, u32[]{:S(2)}) collective-permute-start(f32[136,128]{1,0:T(8,128)S(1)} %add.57), channel_id=1, source_target_pairs={{0,1},{1,0},{2,3},{3,2},{4,5},{5,4},{6,7},{7,6},{8,9},{9,8},{10,11... | collective-permute-start | bytes 208904 | tf_op jit(solution)/shard_map/ppermute | solution.py:361
  117.4 2.7 %collective-permute-done.18 = f32[136,128]{1,0:T(8,128)S(1)} collective-permute-done((f32[136,128]{1,0:T(8,128)S(1)}, f32[136,128]{1,0:T(8,128)S(1)}, u32[]{:S(2)}, u32[]{:S(2)}) %collective-permute-start.18) | collective-permute-done | bytes 69664 | tf_op jit(solution)/shard_map/ppermute | solution.py:361
  120.1 2.1 %collective-permute-start.19 = (f32[136,128]{1,0:T(8,128)S(1)}, f32[136,128]{1,0:T(8,128)S(1)}, u32[]{:S(2)}, u32[]{:S(2)}) collective-permute-start(f32[136,128]{1,0:T(8,128)S(1)} %add.58), channel_id=1, source_target_pairs={{0,2},{1,3},{2,0},{3,1},{4,6},{5,7},{6,4},{7,5},{8,10},{9,11},{10,... | collective-permute-start | bytes 208904 | tf_op jit(solution)/shard_map/ppermute | solution.py:361
  122.2 2.4 %collective-permute-done.19 = f32[136,128]{1,0:T(8,128)S(1)} collective-permute-done((f32[136,128]{1,0:T(8,128)S(1)}, f32[136,128]{1,0:T(8,128)S(1)}, u32[]{:S(2)}, u32[]{:S(2)}) %collective-permute-start.19) | collective-permute-done | bytes 69664 | tf_op jit(solution)/shard_map/ppermute | solution.py:361
  124.7 2.0 %collective-permute-start.20 = (f32[136,128]{1,0:T(8,128)S(1)}, f32[136,128]{1,0:T(8,128)S(1)}, u32[]{:S(2)}, u32[]{:S(2)}) collective-permute-start(f32[136,128]{1,0:T(8,128)S(1)} %add.59), channel_id=1, source_target_pairs={{0,4},{1,5},{2,6},{3,7},{4,0},{5,1},{6,2},{7,3},{8,12},{9,13},{10,... | collective-permute-start | bytes 208904 | tf_op jit(solution)/shard_map/ppermute | solution.py:361
  126.6 3.3 %collective-permute-done.20 = f32[136,128]{1,0:T(8,128)S(1)} collective-permute-done((f32[136,128]{1,0:T(8,128)S(1)}, f32[136,128]{1,0:T(8,128)S(1)}, u32[]{:S(2)}, u32[]{:S(2)}) %collective-permute-start.20) | collective-permute-done | bytes 69664 | tf_op jit(solution)/shard_map/ppermute | solution.py:361
  129.9 0.1 collective-permute-start.21
  130.0 1.2 collective-permute-done.21.theirs_ref
  131.3 9.0 %factor.3.inverse = f32[256,256]{1,0:T(8,128)S(1)} custom-call(s32[1]{0:T(128)} %bitcast.side_ref, f32[136,128]{1,0:T(8,128)S(1)} %add.60.mine_ref, f32[136,128]{1,0:T(8,128)S(1)} %collective-permute-done.21.theirs_ref), custom_call_target="tpu_custom_call" | custom-call | flops 40000000 | bytes 524288 | tf_op jit(solution)/shard_map/factor/pallas_call | solution.py:201
  140.3 3.3 %last.1 = f32[2048,256]{1,0:T(8,128)} custom-call(f32[256,256]{1,0:T(8,128)S(1)} %factor.3.inverse, f32[2048,256]{1,0:T(8,128)S(1)} %get-tuple-element.42.image_ref), custom_call_target="tpu_custom_call" | custom-call | flops 1073741824 | bytes 4194304 | tf_op jit(solution)/shard_map/last/pallas_call | solution.py:254
  (48 shorter events, 0.3 us)
Async XLA Ops:
  2.8 20.5 %collective-permute-start = (f32[48,256]{1,0:T(8,128)S(1)}, f32[48,256]{1,0:T(8,128)S(1)}, u32[]{:S(2)}, u32[]{:S(2)}) collective-permute-start(f32[48,256]{1,0:T(8,128)S(1)} %fusion.refs_0_), channel_id=1, source_target_pairs={{0,4},{1,5},{2,6},{3,7},{4,0},{5,1},{6,2},{7,3},{8,12},{9,13},{10,... | collective-permute-start | bytes 147464 | tf_op jit(solution)/shard_map/ppermute | solution.py:361
  13.9 0.8 copy-start.10
  14.6 5.6 %copy-start.13 = (s32[4,1,8]{2,1,0:T(1,128)S(1)}, s32[4,1,8]{2,1,0:T(1,128)}, u32[]{:S(2)}) copy-start(s32[4,1,8]{2,1,0:T(1,128)} %param.9) | copy-start | bytes 388
  19.5 0.8 copy-start.1
  23.4 4.7 %collective-permute-start.1 = (f32[96,256]{1,0:T(8,128)S(1)}, f32[96,256]{1,0:T(8,128)S(1)}, u32[]{:S(2)}, u32[]{:S(2)}) collective-permute-start(f32[96,256]{1,0:T(8,128)S(1)} %pad_maximum_fusion.2), channel_id=1, source_target_pairs={{0,2},{1,3},{2,0},{3,1},{4,6},{5,7},{6,4},{7,5},{8,10},{9,11},{10,... | collective-permute-start | bytes 294920 | tf_op jit(solution)/shard_map/ppermute | solution.py:361
  28.1 5.7 %collective-permute-start.2 = (f32[192,256]{1,0:T(8,128)S(1)}, f32[192,256]{1,0:T(8,128)S(1)}, u32[]{:S(2)}, u32[]{:S(2)}) collective-permute-start(f32[192,256]{1,0:T(8,128)S(1)} %pad_maximum_fusion), channel_id=1, source_target_pairs={{0,1},{1,0},{2,3},{3,2},{4,5},{5,4},{6,7},{7,6},{8,9},{9,8},{10,11... | collective-permute-start | bytes 589832 | tf_op jit(solution)/shard_map/ppermute | solution.py:361
  30.8 4.2 %copy-start.8 = (f32[192,384]{1,0:T(8,128)}, f32[192,384]{1,0:T(8,128)S(1)}, u32[]{:S(2)}) copy-start(f32[192,384]{1,0:T(8,128)S(1)} %bitcast_multiply_fusion.masked_ref) | copy-start | bytes 884740
  34.9 7.2 %collective-permute-start.3 = (f32[96,256]{1,0:T(8,128)S(1)}, f32[96,256]{1,0:T(8,128)S(1)}, u32[]{:S(2)}, u32[]{:S(2)}) collective-permute-start(f32[96,256]{1,0:T(8,128)S(1)} %get-tuple-element.25), channel_id=1, source_target_pairs={{0,16},{8,24},{16,0},{24,8},{1,17},{9,25},{17,1},{25,9},{2,18},{10... | collective-permute-start | bytes 294920 | tf_op jit(solution)/shard_map/ppermute | solution.py:361
  41.3 0.8 copy-start.3
  42.1 0.6 copy-start.12
  43.4 6.5 %copy-start.7 = (f32[1,48,2048]{2,1,0:T(8,128)S(1)}, f32[1,48,2048]{2,1,0:T(8,128)}, u32[]{:S(2)}) copy-start(f32[1,48,2048]{2,1,0:T(8,128)} %param.7) | copy-start | bytes 1179652
  43.4 5.6 %collective-permute-start.4 = (f32[48,256]{1,0:T(8,128)}, f32[48,256]{1,0:T(8,128)}, u32[]{:S(2)}, u32[]{:S(2)}) collective-permute-start(f32[48,256]{1,0:T(8,128)} %slice.17), channel_id=1, source_target_pairs={{0,8},{8,0},{16,24},{24,16},{1,9},{9,1},{17,25},{25,17},{2,10},{10... | collective-permute-start | bytes 147464 | tf_op jit(solution)/shard_map/ppermute | solution.py:361
  48.2 0.8 copy-start.5
  49.9 1.0 copy-start.2
  50.9 1.0 copy-start.4
  51.9 1.0 copy-start.6
  53.0 1.0 copy-start.11
  56.3 1.3 copy-start
  57.6 5.0 %collective-permute-start.11 = (f32[48,256]{1,0:T(8,128)S(1)}, f32[48,256]{1,0:T(8,128)S(1)}, u32[]{:S(2)}, u32[]{:S(2)}) collective-permute-start(f32[48,256]{1,0:T(8,128)S(1)} %get-tuple-element.32.refs_0_), channel_id=1, source_target_pairs={{0,4},{1,5},{2,6},{3,7},{4,0},{5,1},{6,2},{7,3},{8,12},{9,13},{10,... | collective-permute-start | bytes 147464 | tf_op jit(solution)/shard_map/ppermute | solution.py:361
  57.9 6.4 %collective-permute-start.5 = (f32[136,128]{1,0:T(8,128)S(1)}, f32[136,128]{1,0:T(8,128)S(1)}, u32[]{:S(2)}, u32[]{:S(2)}) collective-permute-start(f32[136,128]{1,0:T(8,128)S(1)} %get-tuple-element.31), channel_id=1, source_target_pairs={{0,8},{8,0},{16,24},{24,16},{1,9},{9,1},{17,25},{25,17},{2,10},{10... | collective-permute-start | bytes 208904 | tf_op jit(solution)/shard_map/ppermute | solution.py:361
  62.6 7.7 %collective-permute-start.12 = (f32[96,256]{1,0:T(8,128)S(1)}, f32[96,256]{1,0:T(8,128)S(1)}, u32[]{:S(2)}, u32[]{:S(2)}) collective-permute-start(f32[96,256]{1,0:T(8,128)S(1)} %pad_maximum_fusion.3), channel_id=1, source_target_pairs={{0,2},{1,3},{2,0},{3,1},{4,6},{5,7},{6,4},{7,5},{8,10},{9,11},{10,... | collective-permute-start | bytes 294920 | tf_op jit(solution)/shard_map/ppermute | solution.py:361
  64.3 4.4 %collective-permute-start.6 = (f32[136,128]{1,0:T(8,128)S(1)}, f32[136,128]{1,0:T(8,128)S(1)}, u32[]{:S(2)}, u32[]{:S(2)}) collective-permute-start(f32[136,128]{1,0:T(8,128)S(1)} %add.49), channel_id=1, source_target_pairs={{0,16},{8,24},{16,0},{24,8},{1,17},{9,25},{17,1},{25,9},{2,18},{10... | collective-permute-start | bytes 208904 | tf_op jit(solution)/shard_map/ppermute | solution.py:361
  68.7 5.1 %collective-permute-start.7 = (f32[136,128]{1,0:T(8,128)S(1)}, f32[136,128]{1,0:T(8,128)S(1)}, u32[]{:S(2)}, u32[]{:S(2)}) collective-permute-start(f32[136,128]{1,0:T(8,128)S(1)} %add.50), channel_id=1, source_target_pairs={{0,1},{1,0},{2,3},{3,2},{4,5},{5,4},{6,7},{7,6},{8,9},{9,8},{10,11... | collective-permute-start | bytes 208904 | tf_op jit(solution)/shard_map/ppermute | solution.py:361
  70.3 11.7 %collective-permute-start.13 = (f32[192,256]{1,0:T(8,128)S(1)}, f32[192,256]{1,0:T(8,128)S(1)}, u32[]{:S(2)}, u32[]{:S(2)}) collective-permute-start(f32[192,256]{1,0:T(8,128)S(1)} %pad_maximum_fusion.1), channel_id=1, source_target_pairs={{0,1},{1,0},{2,3},{3,2},{4,5},{5,4},{6,7},{7,6},{8,9},{9,8},{10,11... | collective-permute-start | bytes 589832 | tf_op jit(solution)/shard_map/ppermute | solution.py:361
  73.8 7.2 %collective-permute-start.8 = (f32[136,128]{1,0:T(8,128)S(1)}, f32[136,128]{1,0:T(8,128)S(1)}, u32[]{:S(2)}, u32[]{:S(2)}) collective-permute-start(f32[136,128]{1,0:T(8,128)S(1)} %add.51), channel_id=1, source_target_pairs={{0,2},{1,3},{2,0},{3,1},{4,6},{5,7},{6,4},{7,5},{8,10},{9,11},{10,... | collective-permute-start | bytes 208904 | tf_op jit(solution)/shard_map/ppermute | solution.py:361
  74.2 7.8 %copy-start.9 = (f32[192,384]{1,0:T(8,128)S(1)}, f32[192,384]{1,0:T(8,128)}, u32[]{:S(2)}) copy-start(f32[192,384]{1,0:T(8,128)} %copy-done.8) | copy-start | bytes 884740
  81.0 8.9 %collective-permute-start.9 = (f32[136,128]{1,0:T(8,128)S(1)}, f32[136,128]{1,0:T(8,128)S(1)}, u32[]{:S(2)}, u32[]{:S(2)}) collective-permute-start(f32[136,128]{1,0:T(8,128)S(1)} %add.52), channel_id=1, source_target_pairs={{0,4},{1,5},{2,6},{3,7},{4,0},{5,1},{6,2},{7,3},{8,12},{9,13},{10,... | collective-permute-start | bytes 208904 | tf_op jit(solution)/shard_map/ppermute | solution.py:361
  83.1 6.8 %collective-permute-start.14 = (f32[96,256]{1,0:T(8,128)S(1)}, f32[96,256]{1,0:T(8,128)S(1)}, u32[]{:S(2)}, u32[]{:S(2)}) collective-permute-start(f32[96,256]{1,0:T(8,128)S(1)} %get-tuple-element.34), channel_id=1, source_target_pairs={{0,16},{8,24},{16,0},{24,8},{1,17},{9,25},{17,1},{25,9},{2,18},{10... | collective-permute-start | bytes 294920 | tf_op jit(solution)/shard_map/ppermute | solution.py:361
  89.9 6.9 %collective-permute-start.10 = (f32[136,128]{1,0:T(8,128)S(1)}, f32[136,128]{1,0:T(8,128)S(1)}, u32[]{:S(2)}, u32[]{:S(2)}) collective-permute-start(f32[136,128]{1,0:T(8,128)S(1)} %add.53.mine_ref), channel_id=1, source_target_pairs={{0,8},{8,0},{16,24},{24,16},{1,9},{9,1},{17,25},{25,17},{2,10},{10... | collective-permute-start | bytes 208904 | tf_op jit(solution)/shard_map/ppermute | solution.py:361
  90.0 15.6 %collective-permute-start.15 = (f32[48,256]{1,0:T(8,128)S(1)}, f32[48,256]{1,0:T(8,128)S(1)}, u32[]{:S(2)}, u32[]{:S(2)}) collective-permute-start(f32[48,256]{1,0:T(8,128)S(1)} %slice.19), channel_id=1, source_target_pairs={{0,8},{8,0},{16,24},{24,16},{1,9},{9,1},{17,25},{25,17},{2,10},{10... | collective-permute-start | bytes 147464 | tf_op jit(solution)/shard_map/ppermute | solution.py:361
  110.0 1.3 collective-permute-start.16
  111.4 4.4 %collective-permute-start.17 = (f32[136,128]{1,0:T(8,128)S(1)}, f32[136,128]{1,0:T(8,128)S(1)}, u32[]{:S(2)}, u32[]{:S(2)}) collective-permute-start(f32[136,128]{1,0:T(8,128)S(1)} %add.56), channel_id=1, source_target_pairs={{0,16},{8,24},{16,0},{24,8},{1,17},{9,25},{17,1},{25,9},{2,18},{10... | collective-permute-start | bytes 208904 | tf_op jit(solution)/shard_map/ppermute | solution.py:361
  115.8 4.4 %collective-permute-start.18 = (f32[136,128]{1,0:T(8,128)S(1)}, f32[136,128]{1,0:T(8,128)S(1)}, u32[]{:S(2)}, u32[]{:S(2)}) collective-permute-start(f32[136,128]{1,0:T(8,128)S(1)} %add.57), channel_id=1, source_target_pairs={{0,1},{1,0},{2,3},{3,2},{4,5},{5,4},{6,7},{7,6},{8,9},{9,8},{10,11... | collective-permute-start | bytes 208904 | tf_op jit(solution)/shard_map/ppermute | solution.py:361
  120.1 4.5 %collective-permute-start.19 = (f32[136,128]{1,0:T(8,128)S(1)}, f32[136,128]{1,0:T(8,128)S(1)}, u32[]{:S(2)}, u32[]{:S(2)}) collective-permute-start(f32[136,128]{1,0:T(8,128)S(1)} %add.58), channel_id=1, source_target_pairs={{0,2},{1,3},{2,0},{3,1},{4,6},{5,7},{6,4},{7,5},{8,10},{9,11},{10,... | collective-permute-start | bytes 208904 | tf_op jit(solution)/shard_map/ppermute | solution.py:361
  124.7 5.3 %collective-permute-start.20 = (f32[136,128]{1,0:T(8,128)S(1)}, f32[136,128]{1,0:T(8,128)S(1)}, u32[]{:S(2)}, u32[]{:S(2)}) collective-permute-start(f32[136,128]{1,0:T(8,128)S(1)} %add.59), channel_id=1, source_target_pairs={{0,4},{1,5},{2,6},{3,7},{4,0},{5,1},{6,2},{7,3},{8,12},{9,13},{10,... | collective-permute-start | bytes 208904 | tf_op jit(solution)/shard_map/ppermute | solution.py:361
  129.9 1.3 collective-permute-start.21
where the time goes:
time: 144 us
  Pallas kernels  70.4 us (49%)
  waiting for transfers between devices  30.9 us (21%)
  starting transfers between devices  23.9 us (17%)
  local copies, waits for them, and re-layouts  13 us (9%)
  matrix products  2.84 us (2%)
  other arithmetic  2.17 us (2%)
    ppermute x22, waiting for transfers between devices, swap(): lax.ppermute(x, axis, [(i, i ^ bit) for i in range(lax.axis_size(axis))])  30.9 us
    pallas_call x5, Pallas kernels, near_of(): pl.pallas_call(functools.partial(near_next_kernel, start), out_shape=out,...  26.8 us
    ppermute x22, starting transfers between devices, swap(): lax.ppermute(x, axis, [(i, i ^ bit) for i in range(lax.axis_size(axis))])  23.9 us
    pallas_call x2, Pallas kernels, factor(): pl.pallas_call(functools.partial(factor_kernel, scale), out_shape=jax.Sha...  17.9 us
    pallas_call x2, Pallas kernels, near_of(): pl.pallas_call(near_first_kernel, out_shape=(out, term, term, term), in_s...  13.7 us
    unnamed x28, local copies, waits for them, and re-layouts  9.27 us
    pallas_call x1, Pallas kernels, middle(): pl.pallas_call(middle_kernel, out_shape=(jax.ShapeDtypeStruct((rows, mode...  4.39 us
    pallas_call x1, Pallas kernels, last(): pl.pallas_call(last_kernel, out_shape=jax.ShapeDtypeStruct(image.shape, j...  3.32 us
  transfers between devices with their start and end apart: 22, of which 11 were waited for; matrix products, arithmetic and copies ran while one was open for 3% of the time, Pallas kernels for 35%

commit v1 on v0

--- a/solution.py
+++ b/solution.py
@@ -153,8 +153,16 @@
         start += piece.shape[0]
 
 
+def project(two, terms):
+    width = two.shape[0] // 2
+    high, mid, low = terms
+    both = mul(two, high) + mul(two, mid)
+    return both[:width] + both[width:] + mul(two[:width], low)
+
+
 def mix_kernel(side_ref, basis_ref, summed_ref, *refs):
-    pieces, (image_ref, coeffs_ref, mine_ref, theirs_ref, stacked, total, cross, parts) = refs[:-8], refs[-8:]
+    pieces, outs = refs[:-10], refs[-10:]
+    high_ref, mid_ref, low_ref, coeffs_ref, mine_ref, theirs_ref, stacked, total, cross, parts = outs
     width = basis_ref.shape[0]
     stack_basis(basis_ref, stacked)
     sums = stack_sums(summed_ref)
@@ -163,14 +171,12 @@
     parts[...] = jnp.zeros_like(parts)
 
     def step(rows, piece):
-        image = piece[...] + mul(stacked[:, rows], sums, (0, 0))
-        image_ref[rows, :] = image
-        high, mid, low = split(image, 3)
+        terms = split(piece[...] + mul(stacked[:, rows], sums, (0, 0)), 3)
+        high, mid, _ = terms
+        high_ref[rows, :], mid_ref[rows, :], low_ref[rows, :] = terms
         total[...] += mul(high, high, (0, 0)) + mul(mid, mid, (0, 0))
         cross[...] += mul(high, mid, (0, 0))
-        two = stacked[: 2 * width, rows]
-        both = mul(two, high) + mul(two, mid)
-        parts[...] += both[:width] + both[width:] + mul(two[:width], low)
+        parts[...] += project(stacked[: 2 * width, rows], terms)
 
     piece_rows(pieces, step)
     coeffs_ref[...] = parts[...]
@@ -182,10 +188,11 @@
     width = basis.shape[0]
     part = jax.ShapeDtypeStruct((modes // 2 + 8, modes // 2), jnp.float32)
     square = pltpu.VMEM((modes, modes), jnp.float32)
+    term = jax.ShapeDtypeStruct((rows, modes), jnp.bfloat16)
     return pl.pallas_call(
         mix_kernel,
-        out_shape=(jax.ShapeDtypeStruct((rows, modes), jnp.float32), jax.ShapeDtypeStruct((width, modes), jnp.float32), part, part),
-        in_specs=[SMEM, VMEM, VMEM] + [VMEM] * len(pieces), out_specs=(VMEM,) * 4,
+        out_shape=(term, term, term, jax.ShapeDtypeStruct((width, modes), jnp.float32), part, part),
+        in_specs=[SMEM, VMEM, VMEM] + [VMEM] * len(pieces), out_specs=(VMEM,) * 6,
         scratch_shapes=[pltpu.VMEM((5 * width, rows), jnp.bfloat16), square, square, pltpu.VMEM((width, modes), jnp.float32)],
         name="mix", compiler_params=pltpu.CompilerParams(vmem_limit_bytes=24 * 2**20), cost_estimate=pl.CostEstimate(flops=12 * rows * modes * modes, bytes_accessed=8 * rows * modes, transcendentals=0),
     )(side, basis, summed, *pieces)
@@ -264,7 +271,7 @@
 TWO = (2, 3, 3)
 
 
-def near_rows(start, dense_ref, high, mid, low, out_ref, held, sems):
+def near_kernel(start, dense_ref, high, mid, low, out_ref, held, sems):
     count = out_ref.shape[0] // BLOCK
 
     def copy(at):
@@ -272,13 +279,17 @@
 
     for at in range(count):
         copy(at).start()
+    row, col = triangle_masks(BLOCK)
 
     def run(at, carry):
         copy(at).wait()
         top, rest = split(held[at], 2)
-        out_ref[pl.ds(pl.multiple_of(at * BLOCK, BLOCK), BLOCK)] = mul(top, high[...]) + (
-            mul(top, mid[...]) + (mul(rest, high[...]) + (mul(rest, mid[...]) + mul(top, low[...])))
-        )
+        out = mul(top, high[...]) + (mul(top, mid[...]) + (mul(rest, high[...]) + mul(top, low[...])))
+        rows = pl.ds(pl.multiple_of(start + at * BLOCK, BLOCK), BLOCK)
+        own = held[at, :, rows]
+        own = jnp.where(row == col, own - own.astype(jnp.bfloat16).astype(jnp.float32), 0.0)
+        out = out + jnp.sum(own, axis=1, keepdims=True) * mid[rows, :].astype(jnp.float32)
+        out_ref[pl.ds(pl.multiple_of(at * BLOCK, BLOCK), BLOCK)] = out
         return carry
 
     lax.fori_loop(0, count, run, 0)
@@ -291,38 +302,34 @@
         return carry
 
     lax.fori_loop(0, field_ref.shape[0] // BLOCK, run, 0)
-    near_rows(0, dense_ref, high, mid, low, out_ref, held, sems)
-
-
-def near_next_kernel(start, dense_ref, high, mid, low, out_ref, held, sems):
-    near_rows(start, dense_ref, high, mid, low, out_ref, held, sems)
-
-
-def near_of(dense, field, shares):
+    near_kernel(0, dense_ref, high, mid, low, out_ref, held, sems)
+
+
+def near_of(dense, field, terms, shares):
     rows, depth = dense.shape
-    modes = field.shape[1]
-    sizes = [rows * share // sum(shares) for share in shares]
-    term = jax.ShapeDtypeStruct(field.shape, jnp.bfloat16)
-    anywhere = pl.BlockSpec(memory_space=pltpu.HBM)
-    pieces, terms, start = [], (), 0
-    for at, size in enumerate(sizes):
+    modes = (terms[0] if terms else field).shape[1]
+    pieces, start = [], 0
+    for share in shares:
+        size = rows * share // sum(shares)
+        count = size // BLOCK
         out = jax.ShapeDtypeStruct((size, modes), jnp.float32)
-        count = size // BLOCK
         settings = dict(
             scratch_shapes=[pltpu.VMEM((count, BLOCK, depth), jnp.float32), pltpu.SemaphoreType.DMA((count,))],
             compiler_params=pltpu.CompilerParams(vmem_limit_bytes=50 * 2**20),
-            cost_estimate=pl.CostEstimate(flops=10 * size * depth * modes, bytes_accessed=4 * size * depth, transcendentals=0),
+            cost_estimate=pl.CostEstimate(flops=8 * size * depth * modes, bytes_accessed=4 * size * depth, transcendentals=0),
         )
-        if at == 0:
+        dense_spec = pl.BlockSpec(memory_space=pltpu.HBM)
+        if terms:
+            piece = pl.pallas_call(
+                functools.partial(near_kernel, start), out_shape=out, in_specs=[dense_spec, VMEM, VMEM, VMEM],
+                out_specs=VMEM, name="near", **settings,
+            )(dense, *terms)
+        else:
+            term = jax.ShapeDtypeStruct(field.shape, jnp.bfloat16)
             piece, *terms = pl.pallas_call(
-                near_first_kernel, out_shape=(out, term, term, term), in_specs=[anywhere, VMEM], out_specs=(VMEM,) * 4,
-                name="near_first", **settings,
+                near_first_kernel, out_shape=(out, term, term, term), in_specs=[dense_spec, VMEM],
+                out_specs=(VMEM,) * 4, name="near_first", **settings,
             )(dense, field)
-        else:
-            piece = pl.pallas_call(
-                functools.partial(near_next_kernel, start), out_shape=out, in_specs=[anywhere, VMEM, VMEM, VMEM],
-                out_specs=VMEM, name="near_next", **settings,
-            )(dense, *terms)
         pieces.append(piece)
         start += size
     return pieces
@@ -406,10 +413,10 @@
         return mine, swap(mine, "grp", 1)
 
     summed = couple_all(jnp.dot(rows_basis, start_block, precision=HP))
-    image, coeffs, mine, theirs = mix(side, near_of(dense, start_block, ONE), rows_basis, summed)
+    *terms, coeffs, mine, theirs = mix(side, near_of(dense, start_block, None, ONE), rows_basis, summed)
     mine, theirs = add_devices(mine, theirs)
     summed = couple_all(coeffs)
-    image, mine, theirs = middle(side, factor(side, mine, theirs, scale), near_of(dense, image, TWO), rows_basis, summed)
+    image, mine, theirs = middle(side, factor(side, mine, theirs, scale), near_of(dense, None, terms, TWO), rows_basis, summed)
     mine, theirs = add_devices(mine, theirs)
     return last(factor(side, mine, theirs, scale), image)
 

time: 144 us -> 128 us (0.89)
  Pallas kernels: 70.4 us -> 64 us
  local copies, waits for them, and re-layouts: 13 us -> 7.61 us
  waiting for transfers between devices: 30.9 us -> 28.3 us
    pallas_call x2 -> x1, Pallas kernels: 13.7 us -> 6.36 us  [near_of(): pl.pallas_call(near_first_kernel, out_shape=(out, term, term, term), in_s...]
    mul x2, local copies, waits for them, and re-layouts: 3.1 us -> 0.37 us  [body(): coupling.reshape(groups, width, span, width) * flags]
    unnamed x28, local copies, waits for them, and re-layouts: 9.27 us -> 6.55 us
    ppermute x22, waiting for transfers between devices: 30.9 us -> 28.3 us  [swap(): lax.ppermute(x, axis, [(i, i ^ bit) for i in range(lax.axis_size(axis))])]
    pallas_call x6 -> x7, Pallas kernels: 29.1 us -> 30 us  [the longest x6 27.7 us: near_of(): pl.pallas_call(functools.partial(near_kernel, start), out_shape=out, in_s...]
  transfers between devices with their start and end apart: 22 -> 22, of which waited for: 11 -> 10; matrix products, arithmetic and copies ran while one was open for 3% -> 0% of each run, Pallas kernels for 35% -> 34%
where the time goes in v1:
time: 128 us
  Pallas kernels  64 us (50%)
  waiting for transfers between devices  28.3 us (22%)
  starting transfers between devices  23.6 us (18%)
  local copies, waits for them, and re-layouts  7.61 us (6%)
  matrix products  2.87 us (2%)
    ppermute x22, waiting for transfers between devices, swap(): lax.ppermute(x, axis, [(i, i ^ bit) for i in range(lax.axis_size(axis))])  28.3 us
    pallas_call x6, Pallas kernels, near_of(): pl.pallas_call(functools.partial(near_kernel, start), out_shape=out, in_s...  27.7 us
    ppermute x22, starting transfers between devices, swap(): lax.ppermute(x, axis, [(i, i ^ bit) for i in range(lax.axis_size(axis))])  23.6 us
    pallas_call x2, Pallas kernels, factor(): pl.pallas_call(functools.partial(factor_kernel, scale), out_shape=jax.Sha...  17.9 us
    unnamed x28, local copies, waits for them, and re-layouts  6.55 us
    pallas_call x1, Pallas kernels, near_of(): pl.pallas_call(near_first_kernel, out_shape=(out, term, term, term), in_s...  6.36 us
    pallas_call x1, Pallas kernels, middle(): pl.pallas_call(middle_kernel, out_shape=(jax.ShapeDtypeStruct((rows, mode...  4.39 us
    pallas_call x1, Pallas kernels, last(): pl.pallas_call(last_kernel, out_shape=jax.ShapeDtypeStruct(image.shape, j...  3.32 us
  transfers between devices with their start and end apart: 22, of which 10 were waited for; matrix products, arithmetic and copies ran while one was open for 0% of the time, Pallas kernels for 34%

profile of v1, /device:TPU:0, one launch (start us, length us, event | category | flops | bytes accessed | tf_op | source)
XLA Modules:
  0.0 128.0 jit_solution(571840402614252827)
XLA Ops:
  0.0 2.9 %fusion.refs_0_ = f32[48,256]{1,0:T(8,128)S(1)} fusion(f32[2048,256]{1,0:T(8,128)} %field_ref.1, f32[1,48,2048]{2,1,0:T(8,128)} %param.7), kind=kOutput, calls=%fused_computation.8 | convolution fusion | flops 301989888 | bytes 2539520 | tf_op jit(solution)/shard_map/dot_general | solution.py:415
  2.9 4.1 %collective-permute-start = (f32[48,256]{1,0:T(8,128)S(1)}, f32[48,256]{1,0:T(8,128)S(1)}, u32[]{:S(2)}, u32[]{:S(2)}) collective-permute-start(f32[48,256]{1,0:T(8,128)S(1)} %fusion.refs_0_), channel_id=1, source_target_pairs={{0,4},{1,5},{2,6},{3,7},{4,0},{5,1},{6,2},{7,3},{8,12},{9,13},{10,... | collective-permute-start | bytes 147464 | tf_op jit(solution)/shard_map/ppermute | solution.py:368
  7.0 0.1 mul.14
  7.1 0.3 mul.15
  7.5 6.4 %near_first.1 = (f32[512,256]{1,0:T(8,128)S(1)}, bf16[2048,256]{1,0:T(8,128)(2,1)S(1)}, bf16[2048,256]{1,0:T(8,128)(2,1)S(1)}, bf16[2048,256]{1,0:T(8,128)(2,1)S(1)}) custom-call(f32[2048,2048]{1,0:T(8,128)} %bitcast.15, f32[2048,256]{1,0:T(8,128)} %field_ref.1), custom_call_target="tpu_custom_call" | custom-call | flops 2147483648 | bytes 4194304 | tf_op jit(solution)/shard_map/near_first/pallas_call | solution.py:329
  13.8 0.0 copy-start.9
  13.9 0.8 copy-done.9
  14.7 1.6 %collective-permute-start.1 = (f32[96,256]{1,0:T(8,128)S(1)}, f32[96,256]{1,0:T(8,128)S(1)}, u32[]{:S(2)}, u32[]{:S(2)}) collective-permute-start(f32[96,256]{1,0:T(8,128)S(1)} %pad_maximum_fusion.2), channel_id=1, source_target_pairs={{0,2},{1,3},{2,0},{3,1},{4,6},{5,7},{6,4},{7,5},{8,10},{9,11},{10,... | collective-permute-start | bytes 294920 | tf_op jit(solution)/shard_map/ppermute | solution.py:368
  16.3 0.1 pad_add_fusion.place_ref
  16.4 3.0 %collective-permute-done.1.refs_2_ = f32[96,256]{1,0:T(8,128)S(1)} collective-permute-done((f32[96,256]{1,0:T(8,128)S(1)}, f32[96,256]{1,0:T(8,128)S(1)}, u32[]{:S(2)}, u32[]{:S(2)}) %collective-permute-start.1) | collective-permute-done | bytes 98336 | tf_op jit(solution)/shard_map/ppermute | solution.py:368
  19.4 1.6 %collective-permute-start.2 = (f32[192,256]{1,0:T(8,128)S(1)}, f32[192,256]{1,0:T(8,128)S(1)}, u32[]{:S(2)}, u32[]{:S(2)}) collective-permute-start(f32[192,256]{1,0:T(8,128)S(1)} %pad_maximum_fusion), channel_id=1, source_target_pairs={{0,1},{1,0},{2,3},{3,2},{4,5},{5,4},{6,7},{7,6},{8,9},{9,8},{10,11... | collective-permute-start | bytes 589832 | tf_op jit(solution)/shard_map/ppermute | solution.py:368
  20.9 4.2 %near.8.refs_3_ = f32[512,256]{1,0:T(8,128)S(1)} custom-call(f32[2048,2048]{1,0:T(8,128)} %bitcast.16, bf16[2048,256]{1,0:T(8,128)(2,1)S(1)} %get-tuple-element.25.high, bf16[2048,256]{1,0:T(8,128)(2,1)S(1)} %get-tuple-element.26.mid, bf16[2048,256]{1,0:T(8,128)(2,1)S(1)} %get-tuple-element.27.low), custom_call_target="tpu_custom_call" | custom-call | flops 2147483648 | bytes 4194304 | tf_op jit(solution)/shard_map/near/pallas_call | solution.py:323
  25.2 1.1 couple.2
  26.3 1.6 %collective-permute-start.3 = (f32[96,256]{1,0:T(8,128)S(1)}, f32[96,256]{1,0:T(8,128)S(1)}, u32[]{:S(2)}, u32[]{:S(2)}) collective-permute-start(f32[96,256]{1,0:T(8,128)S(1)} %get-tuple-element.23), channel_id=1, source_target_pairs={{0,16},{8,24},{16,0},{24,8},{1,17},{9,25},{17,1},{25,9},{2,18},{10... | collective-permute-start | bytes 294920 | tf_op jit(solution)/shard_map/ppermute | solution.py:368
  27.8 4.2 %near.7.refs_2_ = f32[512,256]{1,0:T(8,128)S(1)} custom-call(f32[2048,2048]{1,0:T(8,128)} %bitcast.17, bf16[2048,256]{1,0:T(8,128)(2,1)S(1)} %get-tuple-element.25.high, bf16[2048,256]{1,0:T(8,128)(2,1)S(1)} %get-tuple-element.26.mid, bf16[2048,256]{1,0:T(8,128)(2,1)S(1)} %get-tuple-element.27.low), custom_call_target="tpu_custom_call" | custom-call | flops 2147483648 | bytes 4194304 | tf_op jit(solution)/shard_map/near/pallas_call | solution.py:323
  32.0 0.8 copy-done.2
  32.8 0.0 collective-permute-done.3
  32.9 0.7 slice.17
  33.5 4.2 %near.6.refs_1_ = f32[512,256]{1,0:T(8,128)S(1)} custom-call(f32[2048,2048]{1,0:T(8,128)} %bitcast.18, bf16[2048,256]{1,0:T(8,128)(2,1)S(1)} %get-tuple-element.25.high, bf16[2048,256]{1,0:T(8,128)(2,1)S(1)} %get-tuple-element.26.mid, bf16[2048,256]{1,0:T(8,128)(2,1)S(1)} %get-tuple-element.27.low), custom_call_target="tpu_custom_call" | custom-call | flops 2147483648 | bytes 4194304 | tf_op jit(solution)/shard_map/near/pallas_call | solution.py:323
  37.8 0.8 copy-done.4
  38.6 0.8 slice_add_fusion.1.summed_ref
  39.4 1.0 copy-done.1
  40.5 1.0 copy-done.3
  41.5 1.0 copy-done.5
  42.5 1.0 copy-done.10
  43.6 2.3 %mix.1 = (bf16[2048,256]{1,0:T(8,128)(2,1)S(1)}, bf16[2048,256]{1,0:T(8,128)(2,1)S(1)}, bf16[2048,256]{1,0:T(8,128)(2,1)S(1)}, f32[48,256]{1,0:T(8,128)S(1)}, f3...) custom-call(s32[1]{0:T(128)} %bitcast.side_ref, f32[48,2048]{1,0:T(8,128)S(1)} %bitcast.13, ...), custom_call_target="tpu_custom_call" | custom-call | flops 1610612736 | bytes 4194304 | tf_op jit(solution)/shard_map/mix/pallas_call | solution.py:192
  45.9 0.4 collective-permute-start.11
  46.3 0.2 collective-permute-start.5
  46.5 4.5 %collective-permute-done.11.refs_1_ = f32[48,256]{1,0:T(8,128)S(1)} collective-permute-done((f32[48,256]{1,0:T(8,128)S(1)}, f32[48,256]{1,0:T(8,128)S(1)}, u32[]{:S(2)}, u32[]{:S(2)}) %collective-permute-start.11) | collective-permute-done | bytes 49184 | tf_op jit(solution)/shard_map/ppermute | solution.py:368
  51.0 1.7 %collective-permute-start.12 = (f32[96,256]{1,0:T(8,128)S(1)}, f32[96,256]{1,0:T(8,128)S(1)}, u32[]{:S(2)}, u32[]{:S(2)}) collective-permute-start(f32[96,256]{1,0:T(8,128)S(1)} %pad_maximum_fusion.3), channel_id=1, source_target_pairs={{0,2},{1,3},{2,0},{3,1},{4,6},{5,7},{6,4},{7,5},{8,10},{9,11},{10,... | collective-permute-start | bytes 294920 | tf_op jit(solution)/shard_map/ppermute | solution.py:368
  52.7 0.6 collective-permute-start.6
  53.3 3.8 %collective-permute-done.6 = f32[136,128]{1,0:T(8,128)S(1)} collective-permute-done((f32[136,128]{1,0:T(8,128)S(1)}, f32[136,128]{1,0:T(8,128)S(1)}, u32[]{:S(2)}, u32[]{:S(2)}) %collective-permute-start.6) | collective-permute-done | bytes 69664 | tf_op jit(solution)/shard_map/ppermute | solution.py:368
  57.0 1.5 %collective-permute-start.7 = (f32[136,128]{1,0:T(8,128)S(1)}, f32[136,128]{1,0:T(8,128)S(1)}, u32[]{:S(2)}, u32[]{:S(2)}) collective-permute-start(f32[136,128]{1,0:T(8,128)S(1)} %add.50), channel_id=1, source_target_pairs={{0,1},{1,0},{2,3},{3,2},{4,5},{5,4},{6,7},{7,6},{8,9},{9,8},{10,11... | collective-permute-start | bytes 208904 | tf_op jit(solution)/shard_map/ppermute | solution.py:368
  58.6 0.6 collective-permute-start.13
  59.2 2.9 %collective-permute-done.7 = f32[136,128]{1,0:T(8,128)S(1)} collective-permute-done((f32[136,128]{1,0:T(8,128)S(1)}, f32[136,128]{1,0:T(8,128)S(1)}, u32[]{:S(2)}, u32[]{:S(2)}) %collective-permute-start.7) | collective-permute-done | bytes 69664 | tf_op jit(solution)/shard_map/ppermute | solution.py:368
  62.2 0.3 collective-permute-start.8
  62.5 5.4 %near.11.refs_2_ = f32[768,256]{1,0:T(8,128)S(1)} custom-call(f32[2048,2048]{1,0:T(8,128)} %bitcast.19, bf16[2048,256]{1,0:T(8,128)(2,1)S(1)} %get-tuple-element.33.high, bf16[2048,256]{1,0:T(8,128)(2,1)S(1)} %get-tuple-element.34.mid, bf16[2048,256]{1,0:T(8,128)(2,1)S(1)} %get-tuple-element.35.low), custom_call_target="tpu_custom_call" | custom-call | flops 3221225472 | bytes 6291456 | tf_op jit(solution)/shard_map/near/pallas_call | solution.py:323
  67.9 0.0 collective-permute-done.8
  67.9 1.1 collective-permute-start.9
  69.0 0.0 collective-permute-done.13.refs_3_
  69.0 1.1 couple.3
  70.1 0.6 collective-permute-start.14
  70.7 5.4 %near.10.refs_1_ = f32[768,256]{1,0:T(8,128)S(1)} custom-call(f32[2048,2048]{1,0:T(8,128)} %bitcast.20, bf16[2048,256]{1,0:T(8,128)(2,1)S(1)} %get-tuple-element.33.high, bf16[2048,256]{1,0:T(8,128)(2,1)S(1)} %get-tuple-element.34.mid, bf16[2048,256]{1,0:T(8,128)(2,1)S(1)} %get-tuple-element.35.low), custom_call_target="tpu_custom_call" | custom-call | flops 3221225472 | bytes 6291456 | tf_op jit(solution)/shard_map/near/pallas_call | solution.py:323
  76.1 0.0 collective-permute-done.9
  76.1 0.1 collective-permute-start.10
  76.2 0.0 collective-permute-done.14
  76.2 0.5 collective-permute-start.15
  76.8 4.3 %near.9.refs_0_ = f32[512,256]{1,0:T(8,128)S(1)} custom-call(f32[2048,2048]{1,0:T(8,128)} %bitcast.21, bf16[2048,256]{1,0:T(8,128)(2,1)S(1)} %get-tuple-element.33.high, bf16[2048,256]{1,0:T(8,128)(2,1)S(1)} %get-tuple-element.34.mid, bf16[2048,256]{1,0:T(8,128)(2,1)S(1)} %get-tuple-element.35.low), custom_call_target="tpu_custom_call" | custom-call | flops 2147483648 | bytes 4194304 | tf_op jit(solution)/shard_map/near/pallas_call | solution.py:323
  81.1 8.8 %factor.2.inverse = f32[256,256]{1,0:T(8,128)S(1)} custom-call(s32[1]{0:T(128)} %bitcast.side_ref, f32[136,128]{1,0:T(8,128)S(1)} %add.53.mine_ref, f32[136,128]{1,0:T(8,128)S(1)} %collective-permute-done.10.theirs_ref), custom_call_target="tpu_custom_call" | custom-call | flops 40000000 | bytes 524288 | tf_op jit(solution)/shard_map/factor/pallas_call | solution.py:208
  89.9 4.4 %middle.1 = (f32[2048,256]{1,0:T(8,128)S(1)}, f32[136,128]{1,0:T(8,128)S(1)}, f32[136,128]{1,0:T(8,128)S(1)}) custom-call(s32[1]{0:T(128)} %bitcast.side_ref, f32[256,256]{1,0:T(8,128)S(1)} %factor.2.inverse, f32[48,2048]{1,0:T(8,128)S(1)} %bitcast.14, f32[48,256]{1,0:T(8,128)S(1)} %slice_add_fusion.summed_ref, f32[512,256]{1,0:T(8,128)S(1)} %near.9.refs_0_, ...), custom_call_target="tpu_custom_call" | custom-call | flops 2684354560 | bytes 4194304 | tf_op jit(solution)/shard_map/middle/pallas_call | solution.py:241
  94.3 0.1 collective-permute-start.16
  94.4 1.2 collective-permute-done.16
  95.7 1.6 %collective-permute-start.17 = (f32[136,128]{1,0:T(8,128)S(1)}, f32[136,128]{1,0:T(8,128)S(1)}, u32[]{:S(2)}, u32[]{:S(2)}) collective-permute-start(f32[136,128]{1,0:T(8,128)S(1)} %add.56), channel_id=1, source_target_pairs={{0,16},{8,24},{16,0},{24,8},{1,17},{9,25},{17,1},{25,9},{2,18},{10... | collective-permute-start | bytes 208904 | tf_op jit(solution)/shard_map/ppermute | solution.py:368
  97.2 2.8 %collective-permute-done.17 = f32[136,128]{1,0:T(8,128)S(1)} collective-permute-done((f32[136,128]{1,0:T(8,128)S(1)}, f32[136,128]{1,0:T(8,128)S(1)}, u32[]{:S(2)}, u32[]{:S(2)}) %collective-permute-start.17) | collective-permute-done | bytes 69664 | tf_op jit(solution)/shard_map/ppermute | solution.py:368
  100.1 1.5 %collective-permute-start.18 = (f32[136,128]{1,0:T(8,128)S(1)}, f32[136,128]{1,0:T(8,128)S(1)}, u32[]{:S(2)}, u32[]{:S(2)}) collective-permute-start(f32[136,128]{1,0:T(8,128)S(1)} %add.57), channel_id=1, source_target_pairs={{0,1},{1,0},{2,3},{3,2},{4,5},{5,4},{6,7},{7,6},{8,9},{9,8},{10,11... | collective-permute-start | bytes 208904 | tf_op jit(solution)/shard_map/ppermute | solution.py:368
  101.6 2.9 %collective-permute-done.18 = f32[136,128]{1,0:T(8,128)S(1)} collective-permute-done((f32[136,128]{1,0:T(8,128)S(1)}, f32[136,128]{1,0:T(8,128)S(1)}, u32[]{:S(2)}, u32[]{:S(2)}) %collective-permute-start.18) | collective-permute-done | bytes 69664 | tf_op jit(solution)/shard_map/ppermute | solution.py:368
  104.5 2.1 %collective-permute-start.19 = (f32[136,128]{1,0:T(8,128)S(1)}, f32[136,128]{1,0:T(8,128)S(1)}, u32[]{:S(2)}, u32[]{:S(2)}) collective-permute-start(f32[136,128]{1,0:T(8,128)S(1)} %add.58), channel_id=1, source_target_pairs={{0,2},{1,3},{2,0},{3,1},{4,6},{5,7},{6,4},{7,5},{8,10},{9,11},{10,... | collective-permute-start | bytes 208904 | tf_op jit(solution)/shard_map/ppermute | solution.py:368
  106.5 2.5 %collective-permute-done.19 = f32[136,128]{1,0:T(8,128)S(1)} collective-permute-done((f32[136,128]{1,0:T(8,128)S(1)}, f32[136,128]{1,0:T(8,128)S(1)}, u32[]{:S(2)}, u32[]{:S(2)}) %collective-permute-start.19) | collective-permute-done | bytes 69664 | tf_op jit(solution)/shard_map/ppermute | solution.py:368
  109.0 1.8 %collective-permute-start.20 = (f32[136,128]{1,0:T(8,128)S(1)}, f32[136,128]{1,0:T(8,128)S(1)}, u32[]{:S(2)}, u32[]{:S(2)}) collective-permute-start(f32[136,128]{1,0:T(8,128)S(1)} %add.59), channel_id=1, source_target_pairs={{0,4},{1,5},{2,6},{3,7},{4,0},{5,1},{6,2},{7,3},{8,12},{9,13},{10,... | collective-permute-start | bytes 208904 | tf_op jit(solution)/shard_map/ppermute | solution.py:368
  110.8 3.5 %collective-permute-done.20 = f32[136,128]{1,0:T(8,128)S(1)} collective-permute-done((f32[136,128]{1,0:T(8,128)S(1)}, f32[136,128]{1,0:T(8,128)S(1)}, u32[]{:S(2)}, u32[]{:S(2)}) %collective-permute-start.20) | collective-permute-done | bytes 69664 | tf_op jit(solution)/shard_map/ppermute | solution.py:368
  114.3 0.1 collective-permute-start.21
  114.4 1.2 collective-permute-done.21.theirs_ref
  115.6 9.0 %factor.3.inverse = f32[256,256]{1,0:T(8,128)S(1)} custom-call(s32[1]{0:T(128)} %bitcast.side_ref, f32[136,128]{1,0:T(8,128)S(1)} %add.60.mine_ref, f32[136,128]{1,0:T(8,128)S(1)} %collective-permute-done.21.theirs_ref), custom_call_target="tpu_custom_call" | custom-call | flops 40000000 | bytes 524288 | tf_op jit(solution)/shard_map/factor/pallas_call | solution.py:208
  124.7 3.3 %last.1 = f32[2048,256]{1,0:T(8,128)} custom-call(f32[256,256]{1,0:T(8,128)S(1)} %factor.3.inverse, f32[2048,256]{1,0:T(8,128)S(1)} %get-tuple-element.38.image_ref), custom_call_target="tpu_custom_call" | custom-call | flops 1073741824 | bytes 4194304 | tf_op jit(solution)/shard_map/last/pallas_call | solution.py:261
  (48 shorter events, 0.3 us)
Async XLA Ops:
  0.0 7.0 %copy-start.13 = (s32[4,1,8]{2,1,0:T(1,128)S(1)}, s32[4,1,8]{2,1,0:T(1,128)}, u32[]{:S(2)}) copy-start(s32[4,1,8]{2,1,0:T(1,128)} %param.9) | copy-start | bytes 388
  0.0 7.4 %copy-start.12 = (f32[4,1,48,384]{3,2,1,0:T(8,128)S(1)}, f32[4,1,48,384]{3,2,1,0:T(8,128)}, u32[]{:S(2)}) copy-start(f32[4,1,48,384]{3,2,1,0:T(8,128)} %param.8) | copy-start | bytes 884740
  2.9 11.8 %collective-permute-start = (f32[48,256]{1,0:T(8,128)S(1)}, f32[48,256]{1,0:T(8,128)S(1)}, u32[]{:S(2)}, u32[]{:S(2)}) collective-permute-start(f32[48,256]{1,0:T(8,128)S(1)} %fusion.refs_0_), channel_id=1, source_target_pairs={{0,4},{1,5},{2,6},{3,7},{4,0},{5,1},{6,2},{7,3},{8,12},{9,13},{10,... | collective-permute-start | bytes 147464 | tf_op jit(solution)/shard_map/ppermute | solution.py:368
  7.5 17.7 %copy-start.7 = (f32[192,384]{1,0:T(8,128)}, f32[192,384]{1,0:T(8,128)S(1)}, u32[]{:S(2)}) copy-start(f32[192,384]{1,0:T(8,128)S(1)} %bitcast_multiply_fusion.masked_ref) | copy-start | bytes 884740
  13.8 0.8 copy-start.9
  14.7 4.7 %collective-permute-start.1 = (f32[96,256]{1,0:T(8,128)S(1)}, f32[96,256]{1,0:T(8,128)S(1)}, u32[]{:S(2)}, u32[]{:S(2)}) collective-permute-start(f32[96,256]{1,0:T(8,128)S(1)} %pad_maximum_fusion.2), channel_id=1, source_target_pairs={{0,2},{1,3},{2,0},{3,1},{4,6},{5,7},{6,4},{7,5},{8,10},{9,11},{10,... | collective-permute-start | bytes 294920 | tf_op jit(solution)/shard_map/ppermute | solution.py:368
  19.4 5.8 %collective-permute-start.2 = (f32[192,256]{1,0:T(8,128)S(1)}, f32[192,256]{1,0:T(8,128)S(1)}, u32[]{:S(2)}, u32[]{:S(2)}) collective-permute-start(f32[192,256]{1,0:T(8,128)S(1)} %pad_maximum_fusion), channel_id=1, source_target_pairs={{0,1},{1,0},{2,3},{3,2},{4,5},{5,4},{6,7},{7,6},{8,9},{9,8},{10,11... | collective-permute-start | bytes 589832 | tf_op jit(solution)/shard_map/ppermute | solution.py:368
  25.1 6.9 %copy-start = (f32[512,256]{1,0:T(8,128)}, f32[512,256]{1,0:T(8,128)S(1)}, u32[]{:S(2)}) copy-start(f32[512,256]{1,0:T(8,128)S(1)} %near.8.refs_3_) | copy-start | bytes 1572868
  26.3 6.6 %collective-permute-start.3 = (f32[96,256]{1,0:T(8,128)S(1)}, f32[96,256]{1,0:T(8,128)S(1)}, u32[]{:S(2)}, u32[]{:S(2)}) collective-permute-start(f32[96,256]{1,0:T(8,128)S(1)} %get-tuple-element.23), channel_id=1, source_target_pairs={{0,16},{8,24},{16,0},{24,8},{1,17},{9,25},{17,1},{25,9},{2,18},{10... | collective-permute-start | bytes 294920 | tf_op jit(solution)/shard_map/ppermute | solution.py:368
  32.0 0.8 copy-start.2
  32.8 0.7 copy-start.11
  33.5 5.9 %copy-start.6 = (f32[1,48,2048]{2,1,0:T(8,128)S(1)}, f32[1,48,2048]{2,1,0:T(8,128)}, u32[]{:S(2)}) copy-start(f32[1,48,2048]{2,1,0:T(8,128)} %param.7) | copy-start | bytes 1179652
  33.5 5.0 %collective-permute-start.4 = (f32[48,256]{1,0:T(8,128)}, f32[48,256]{1,0:T(8,128)}, u32[]{:S(2)}, u32[]{:S(2)}) collective-permute-start(f32[48,256]{1,0:T(8,128)} %slice.17), channel_id=1, source_target_pairs={{0,8},{8,0},{16,24},{24,16},{1,9},{9,1},{17,25},{25,17},{2,10},{10... | collective-permute-start | bytes 147464 | tf_op jit(solution)/shard_map/ppermute | solution.py:368
  37.8 0.8 copy-start.4
  39.4 1.0 copy-start.1
  40.5 1.0 copy-start.3
  41.5 1.0 copy-start.5
  42.5 1.0 copy-start.10
  45.9 5.1 %collective-permute-start.11 = (f32[48,256]{1,0:T(8,128)S(1)}, f32[48,256]{1,0:T(8,128)S(1)}, u32[]{:S(2)}, u32[]{:S(2)}) collective-permute-start(f32[48,256]{1,0:T(8,128)S(1)} %get-tuple-element.30.refs_0_), channel_id=1, source_target_pairs={{0,4},{1,5},{2,6},{3,7},{4,0},{5,1},{6,2},{7,3},{8,12},{9,13},{10,... | collective-permute-start | bytes 147464 | tf_op jit(solution)/shard_map/ppermute | solution.py:368
  46.3 6.4 %collective-permute-start.5 = (f32[136,128]{1,0:T(8,128)S(1)}, f32[136,128]{1,0:T(8,128)S(1)}, u32[]{:S(2)}, u32[]{:S(2)}) collective-permute-start(f32[136,128]{1,0:T(8,128)S(1)} %get-tuple-element.29), channel_id=1, source_target_pairs={{0,8},{8,0},{16,24},{24,16},{1,9},{9,1},{17,25},{25,17},{2,10},{10... | collective-permute-start | bytes 208904 | tf_op jit(solution)/shard_map/ppermute | solution.py:368
  51.0 7.6 %collective-permute-start.12 = (f32[96,256]{1,0:T(8,128)S(1)}, f32[96,256]{1,0:T(8,128)S(1)}, u32[]{:S(2)}, u32[]{:S(2)}) collective-permute-start(f32[96,256]{1,0:T(8,128)S(1)} %pad_maximum_fusion.3), channel_id=1, source_target_pairs={{0,2},{1,3},{2,0},{3,1},{4,6},{5,7},{6,4},{7,5},{8,10},{9,11},{10,... | collective-permute-start | bytes 294920 | tf_op jit(solution)/shard_map/ppermute | solution.py:368
  52.7 4.4 %collective-permute-start.6 = (f32[136,128]{1,0:T(8,128)S(1)}, f32[136,128]{1,0:T(8,128)S(1)}, u32[]{:S(2)}, u32[]{:S(2)}) collective-permute-start(f32[136,128]{1,0:T(8,128)S(1)} %add.49), channel_id=1, source_target_pairs={{0,16},{8,24},{16,0},{24,8},{1,17},{9,25},{17,1},{25,9},{2,18},{10... | collective-permute-start | bytes 208904 | tf_op jit(solution)/shard_map/ppermute | solution.py:368
  57.0 5.1 %collective-permute-start.7 = (f32[136,128]{1,0:T(8,128)S(1)}, f32[136,128]{1,0:T(8,128)S(1)}, u32[]{:S(2)}, u32[]{:S(2)}) collective-permute-start(f32[136,128]{1,0:T(8,128)S(1)} %add.50), channel_id=1, source_target_pairs={{0,1},{1,0},{2,3},{3,2},{4,5},{5,4},{6,7},{7,6},{8,9},{9,8},{10,11... | collective-permute-start | bytes 208904 | tf_op jit(solution)/shard_map/ppermute | solution.py:368
  58.6 10.4 %collective-permute-start.13 = (f32[192,256]{1,0:T(8,128)S(1)}, f32[192,256]{1,0:T(8,128)S(1)}, u32[]{:S(2)}, u32[]{:S(2)}) collective-permute-start(f32[192,256]{1,0:T(8,128)S(1)} %pad_maximum_fusion.1), channel_id=1, source_target_pairs={{0,1},{1,0},{2,3},{3,2},{4,5},{5,4},{6,7},{7,6},{8,9},{9,8},{10,11... | collective-permute-start | bytes 589832 | tf_op jit(solution)/shard_map/ppermute | solution.py:368
  62.2 5.7 %collective-permute-start.8 = (f32[136,128]{1,0:T(8,128)S(1)}, f32[136,128]{1,0:T(8,128)S(1)}, u32[]{:S(2)}, u32[]{:S(2)}) collective-permute-start(f32[136,128]{1,0:T(8,128)S(1)} %add.51), channel_id=1, source_target_pairs={{0,2},{1,3},{2,0},{3,1},{4,6},{5,7},{6,4},{7,5},{8,10},{9,11},{10,... | collective-permute-start | bytes 208904 | tf_op jit(solution)/shard_map/ppermute | solution.py:368
  62.5 6.6 %copy-start.8 = (f32[192,384]{1,0:T(8,128)S(1)}, f32[192,384]{1,0:T(8,128)}, u32[]{:S(2)}) copy-start(f32[192,384]{1,0:T(8,128)} %copy-done.7) | copy-start | bytes 884740
  67.9 8.2 %collective-permute-start.9 = (f32[136,128]{1,0:T(8,128)S(1)}, f32[136,128]{1,0:T(8,128)S(1)}, u32[]{:S(2)}, u32[]{:S(2)}) collective-permute-start(f32[136,128]{1,0:T(8,128)S(1)} %add.52), channel_id=1, source_target_pairs={{0,4},{1,5},{2,6},{3,7},{4,0},{5,1},{6,2},{7,3},{8,12},{9,13},{10,... | collective-permute-start | bytes 208904 | tf_op jit(solution)/shard_map/ppermute | solution.py:368
  70.1 6.1 %collective-permute-start.14 = (f32[96,256]{1,0:T(8,128)S(1)}, f32[96,256]{1,0:T(8,128)S(1)}, u32[]{:S(2)}, u32[]{:S(2)}) collective-permute-start(f32[96,256]{1,0:T(8,128)S(1)} %get-tuple-element.32), channel_id=1, source_target_pairs={{0,16},{8,24},{16,0},{24,8},{1,17},{9,25},{17,1},{25,9},{2,18},{10... | collective-permute-start | bytes 294920 | tf_op jit(solution)/shard_map/ppermute | solution.py:368
  76.1 5.0 %collective-permute-start.10 = (f32[136,128]{1,0:T(8,128)S(1)}, f32[136,128]{1,0:T(8,128)S(1)}, u32[]{:S(2)}, u32[]{:S(2)}) collective-permute-start(f32[136,128]{1,0:T(8,128)S(1)} %add.53.mine_ref), channel_id=1, source_target_pairs={{0,8},{8,0},{16,24},{24,16},{1,9},{9,1},{17,25},{25,17},{2,10},{10... | collective-permute-start | bytes 208904 | tf_op jit(solution)/shard_map/ppermute | solution.py:368
  76.2 13.7 %collective-permute-start.15 = (f32[48,256]{1,0:T(8,128)S(1)}, f32[48,256]{1,0:T(8,128)S(1)}, u32[]{:S(2)}, u32[]{:S(2)}) collective-permute-start(f32[48,256]{1,0:T(8,128)S(1)} %slice.19), channel_id=1, source_target_pairs={{0,8},{8,0},{16,24},{24,16},{1,9},{9,1},{17,25},{25,17},{2,10},{10... | collective-permute-start | bytes 147464 | tf_op jit(solution)/shard_map/ppermute | solution.py:368
  94.3 1.3 %collective-permute-start.16 = (f32[136,128]{1,0:T(8,128)S(1)}, f32[136,128]{1,0:T(8,128)S(1)}, u32[]{:S(2)}, u32[]{:S(2)}) collective-permute-start(f32[136,128]{1,0:T(8,128)S(1)} %get-tuple-element.37), channel_id=1, source_target_pairs={{0,8},{8,0},{16,24},{24,16},{1,9},{9,1},{17,25},{25,17},{2,10},{10... | collective-permute-start | bytes 208904 | tf_op jit(solution)/shard_map/ppermute | solution.py:368
  95.7 4.4 %collective-permute-start.17 = (f32[136,128]{1,0:T(8,128)S(1)}, f32[136,128]{1,0:T(8,128)S(1)}, u32[]{:S(2)}, u32[]{:S(2)}) collective-permute-start(f32[136,128]{1,0:T(8,128)S(1)} %add.56), channel_id=1, source_target_pairs={{0,16},{8,24},{16,0},{24,8},{1,17},{9,25},{17,1},{25,9},{2,18},{10... | collective-permute-start | bytes 208904 | tf_op jit(solution)/shard_map/ppermute | solution.py:368
  100.1 4.4 %collective-permute-start.18 = (f32[136,128]{1,0:T(8,128)S(1)}, f32[136,128]{1,0:T(8,128)S(1)}, u32[]{:S(2)}, u32[]{:S(2)}) collective-permute-start(f32[136,128]{1,0:T(8,128)S(1)} %add.57), channel_id=1, source_target_pairs={{0,1},{1,0},{2,3},{3,2},{4,5},{5,4},{6,7},{7,6},{8,9},{9,8},{10,11... | collective-permute-start | bytes 208904 | tf_op jit(solution)/shard_map/ppermute | solution.py:368
  104.5 4.6 %collective-permute-start.19 = (f32[136,128]{1,0:T(8,128)S(1)}, f32[136,128]{1,0:T(8,128)S(1)}, u32[]{:S(2)}, u32[]{:S(2)}) collective-permute-start(f32[136,128]{1,0:T(8,128)S(1)} %add.58), channel_id=1, source_target_pairs={{0,2},{1,3},{2,0},{3,1},{4,6},{5,7},{6,4},{7,5},{8,10},{9,11},{10,... | collective-permute-start | bytes 208904 | tf_op jit(solution)/shard_map/ppermute | solution.py:368
  109.0 5.3 %collective-permute-start.20 = (f32[136,128]{1,0:T(8,128)S(1)}, f32[136,128]{1,0:T(8,128)S(1)}, u32[]{:S(2)}, u32[]{:S(2)}) collective-permute-start(f32[136,128]{1,0:T(8,128)S(1)} %add.59), channel_id=1, source_target_pairs={{0,4},{1,5},{2,6},{3,7},{4,0},{5,1},{6,2},{7,3},{8,12},{9,13},{10,... | collective-permute-start | bytes 208904 | tf_op jit(solution)/shard_map/ppermute | solution.py:368
  114.3 1.3 %collective-permute-start.21 = (f32[136,128]{1,0:T(8,128)S(1)}, f32[136,128]{1,0:T(8,128)S(1)}, u32[]{:S(2)}, u32[]{:S(2)}) collective-permute-start(f32[136,128]{1,0:T(8,128)S(1)} %add.60.mine_ref), channel_id=1, source_target_pairs={{0,8},{8,0},{16,24},{24,16},{1,9},{9,1},{17,25},{25,17},{2,10},{10... | collective-permute-start | bytes 208904 | tf_op jit(solution)/shard_map/ppermute | solution.py:368
